TPU v7x, 256 devices: a whole 4x4x8 slice. The times are simulated.
256 devices in a mesh: gx: 64 (over x, z, core), gy: 4 (over y).
Axes of the slice: x: 4, y: 4, z: 8, core: 2. Of those that a mesh axis runs over, the one named last changes fastest.
Arguments:
- measures: bfloat16 [2097152, 128], P(('gx', 'gy')), may hold values from -6 to 6
- row_keys: int32 [2097152], P(('gx', 'gy')), may hold values from 0 to 131071, as said below
- orders: bfloat16 [131072, 128], P(('gx', 'gy')), may hold values from -6 to 6
- heavy_keys: int32 [512], replicated, may hold values from 0 to 131071, as said below
- key_slot: int32 [131072], replicated, may hold values from 0 to 131071, as said below
Outputs:
- result: bfloat16 [131072, 128], P(('gx', 'gy'))
- heavy_report: bfloat16 [512, 128], P(('gx', 'gy'))
- slot_rows: float32 [131072], P(('gx', 'gy'))
Inputs may be any that keep to these rules, and one draw needn't show every extreme that they name: `heavy_keys`: for each range block d, entries d * 2 to (d + 1) * 2 - 1 are distinct keys of d * 512 to (d + 1) * 512 - 1. `key_slot`: A permutation. Slot s belongs to owner s // 2048 and to quarter (s // 512) % q with q = 4. Key k lies in range block d = k // 512; every range block has exactly 8 keys with slots of each owner, all in quarter d % q. `row_keys`: in the rows of one device, among rows whose key is not heavy, at most 256 have slots of any one owner and at most 64 distinct keys have slots of any one owner; in every device both bounds are reached by some owner.
All inputs are finite; a program needn't handle non-finite values.
Results may differ from a plain program's by a relative error of at most 0.0021.
Values may be sent and summed in bfloat16 or wider, within the bound.
A program may use at most 64 MiB of HBM per device.

v0:
```python
import math

import jax
import jax.numpy as jnp
from jax import lax
from jax.sharding import PartitionSpec as P


def sent_together(arrays, axis, split_dim, concat_dim, along):
    columns = [a.reshape(*a.shape[:along], -1) for a in arrays]
    both = jnp.concatenate(columns, axis=along)
    out, at, gathered = (
        lax.all_to_all(both, axis, split_axis=split_dim, concat_axis=concat_dim, tiled=True),
        0,
        [],
    )
    for a, column in zip(arrays, columns):
        share = out[..., at : at + column.shape[along]]
        gathered.append(share.reshape(*share.shape[:along], *a.shape[along:]))
        at += column.shape[along]
    return tuple(gathered)


def cut_along(x, dim, length):
    shape = x.shape
    pieces = x.reshape(*shape[:dim], length, shape[dim] // length, *shape[dim + 1 :])
    return jnp.moveaxis(pieces, dim, 0)


def summed_on_arrival(x, axis, dim):
    pieces = cut_along(x, dim, lax.axis_size(axis))
    arrived = lax.all_to_all(pieces, axis, split_axis=0, concat_axis=0, tiled=True)
    return arrived.sum(axis=0)


def side_by_side(arrays, axis, dim, along):
    widths = [math.prod(a.shape[along:]) for a in arrays]
    both = jnp.concatenate(
        [a.reshape(*a.shape[:along], w) for a, w in zip(arrays, widths)], axis=along
    )
    out = summed_on_arrival(both, axis, dim)
    pieces = jnp.split(out, [sum(widths[:k]) for k in range(1, len(widths))], axis=along)
    return tuple((b.reshape(*out.shape[:along], *a.shape[along:]) for a, b in zip(arrays, pieces)))


def block_length():
    return 2048


def one_hot_sums(values, targets, labels, weights):
    block_rows = block_length()
    blocks = targets.shape[0] // block_rows
    columns = values.shape[1]
    span = labels.shape[0]
    exact = values.dtype == jnp.float32

    def add_block(running, block_piece):
        block_values, block_targets, block_weights = block_piece
        matches = block_targets[:, None] == labels[None, :]
        onehot = matches.astype(values.dtype)
        if exact:
            product = lax.dot_general(
                onehot,
                block_values,
                (((0,), (0,)), ((), ())),
                precision=lax.Precision.HIGHEST,
                preferred_element_type=jnp.float32,
            )
        else:
            product = lax.dot_general(
                onehot, block_values, (((0,), (0,)), ((), ())), preferred_element_type=jnp.float32
            )
        totals = running[0] + product
        tallies = running[1] + jnp.sum(matches.astype(jnp.float32) * block_weights[:, None], axis=0)
        return ((totals, tallies), jnp.any(matches, axis=1))

    start_state = (jnp.zeros((span, columns), jnp.float32), jnp.zeros((span,), jnp.float32))
    pieces = (
        values.reshape(blocks, block_rows, columns),
        targets.reshape(blocks, block_rows),
        weights.reshape(blocks, block_rows),
    )
    (totals, tallies), matched = lax.scan(add_block, start_state, pieces)
    return (totals, tallies, matched.reshape(-1))


def body(measures, row_keys, orders, heavy_keys, key_slot):
    row_count, columns = measures.shape
    groups_x = lax.axis_size("gx")
    groups_y = lax.axis_size("gy")
    key_dev = orders.shape[0]
    own_slots = key_dev * groups_y
    heavy_total = heavy_keys.shape[0]
    heavy_each = heavy_total // (groups_x * groups_y)
    capacity = max(row_count // 32, 3 * row_count // (4 * groups_x))
    key_capacity = capacity // 4
    index_x = lax.axis_index("gx")
    index_y = lax.axis_index("gy")
    device = index_x * groups_y + index_y
    unit_rows = jnp.ones((row_count,), jnp.float32)
    heavy_part, heavy_count, heavy_flags = one_hot_sums(measures, row_keys, heavy_keys, unit_rows)
    slot_ids = key_slot[row_keys]
    owner_labels = jnp.arange(groups_x + 1, dtype=jnp.int32)
    own_base = index_x * own_slots
    own_labels = jnp.arange(own_slots, dtype=jnp.int32)
    sort_keys = jnp.where(heavy_flags, groups_x * own_slots, slot_ids)
    ordering = jnp.argsort(sort_keys, stable=True)
    sorted_slots = sort_keys[ordering]
    sorted_owner = sorted_slots // own_slots
    is_light = sorted_owner < groups_x
    fresh = (
        jnp.concatenate([jnp.ones((1,), bool), sorted_slots[1:] != sorted_slots[:-1]]) & is_light
    )
    distinct = jnp.cumsum(fresh.astype(jnp.int32)) - 1
    before = jnp.sum(
        (fresh[:, None] & (sorted_owner[:, None] < owner_labels[None, :])).astype(jnp.int32), axis=0
    )
    segments = groups_x * key_capacity
    segment = jnp.where(
        is_light, sorted_owner * key_capacity + distinct - before[sorted_owner], segments
    )
    row_segment = jnp.zeros((row_count,), jnp.int32).at[ordering].set(segment)
    partial_value, tallies, unused = one_hot_sums(
        measures, row_segment, jnp.arange(segments, dtype=jnp.int32), unit_rows
    )
    sent_slots = jnp.full((segments + 1,), -1, jnp.int32).at[segment].set(sorted_slots)[:segments]
    got_sums, got_tallies, got_slots = (
        *sent_together(
            (
                partial_value.reshape(groups_x, key_capacity, columns),
                tallies.reshape(groups_x, key_capacity),
            ),
            "gx",
            0,
            0,
            2,
        ),
        lax.all_to_all(
            sent_slots.reshape(groups_x, key_capacity),
            "gx",
            split_axis=0,
            concat_axis=0,
            tiled=True,
        ),
    )
    local_slot = got_slots.reshape(-1) - own_base
    local_slot = jnp.where(got_slots.reshape(-1) >= 0, local_slot, own_slots)
    light_totals, light_tallies, unused_too = one_hot_sums(
        got_sums.reshape(-1, columns), local_slot, own_labels, got_tallies.reshape(-1)
    )
    quarter_totals, quarter_tallies = side_by_side(
        (
            light_totals.reshape(groups_y, key_dev, columns),
            light_tallies.reshape(groups_y, key_dev),
        ),
        "gy",
        0,
        2,
    )
    slot_rows = quarter_tallies.reshape(key_dev)
    inverse = jnp.argsort(key_slot)
    held_keys = lax.dynamic_slice_in_dim(inverse, device * key_dev, key_dev)
    send_order = jnp.argsort(held_keys)
    per_peer = key_dev // groups_x
    moved_totals, moved_tallies = sent_together(
        (
            quarter_totals.reshape(key_dev, columns)[send_order].reshape(
                groups_x, per_peer, columns
            ),
            slot_rows[send_order].reshape(groups_x, per_peer),
        ),
        "gx",
        0,
        0,
        2,
    )
    range_slots = lax.dynamic_slice_in_dim(key_slot, device * key_dev, key_dev)
    arrival = jnp.argsort(range_slots // own_slots, stable=True)
    placed = jnp.argsort(arrival)
    light_sum = moved_totals.reshape(key_dev, columns)[placed]
    light_count = moved_tallies.reshape(key_dev)[placed]
    my_heavy = lax.dynamic_slice_in_dim(heavy_keys, device * heavy_each, heavy_each)
    heavy_local = my_heavy - device * key_dev
    heavy_orders_here = orders[heavy_local]
    shares, share_count = (
        lax.psum_scatter(heavy_part, ("gx", "gy"), scatter_dimension=0, tiled=True),
        lax.psum_scatter(heavy_count, ("gx", "gy"), scatter_dimension=0, tiled=True),
    )
    heavy_value = (
        heavy_orders_here.astype(jnp.float32) * shares * lax.rsqrt(1.0 + share_count)[:, None]
    )
    light_value = orders.astype(jnp.float32) * light_sum * lax.rsqrt(1.0 + light_count)[:, None]
    placing = (heavy_local[:, None] == jnp.arange(key_dev, dtype=jnp.int32)[None, :]).astype(
        jnp.float32
    )
    heavy_full = jnp.sum(placing[:, :, None] * heavy_value[:, None, :], axis=0)
    result = (light_value + heavy_full).astype(jnp.bfloat16)
    return (result, heavy_value.astype(jnp.bfloat16), slot_rows)


def solution(mesh):
    return jax.shard_map(
        body,
        mesh=mesh,
        in_specs=(P(("gx", "gy"), None), P(("gx", "gy")), P(("gx", "gy"), None), P(), P()),
        out_specs=(P(("gx", "gy"), None), P(("gx", "gy"), None), P(("gx", "gy"))),
        check_vma=False,
    )
```

profile of v0, /device:TPU:1, one launch (start us, length us, event | category | flops | bytes accessed | tf_op | source)
XLA Modules:
  0.0 637.5 jit_solution(5043846318612129661)
XLA Ops:
  9.6 22.6 %while.41 = (s32[]{:T(128)}, f32[512,128]{1,0:T(8,128)S(1)}, f32[512]{0:T(512)S(1)}, pred[4,2048]{1,0:T(4,128)(4,1)S(1)}, s32[4,2048]{1,0:T(4,128)S(1)}, /*index...) while((s32[]{:T(128)}, f32[512,128]{1,0:T(8,128)S(1)}, f32[512]{0:T(512)S(1)}, ...), condition=%wide.region_3.4_spmd.clone, body=%wide.region_0.3_spmd.clone.sunk | while | flops 274856448 | bytes 1114736 | solution.py:83
  9.6 2.7 fusion.66
  13.6 1.5 compare_reduce_fusion.2
  15.3 2.7 fusion.66
  19.2 1.5 compare_reduce_fusion.2
  20.9 2.7 fusion.66
  24.9 1.5 compare_reduce_fusion.2
  26.6 2.7 fusion.66
  30.5 1.5 compare_reduce_fusion.2
  32.2 45.5 %gather_fusion = s32[8192]{0:T(1024)S(1)} fusion(s32[131072]{0:T(1024)S(1)} %copy-done, s32[8192]{0:T(1024)S(1)} %fusion.35), kind=kCustom, calls=%fused_computation | custom fusion | bytes 98304 | tf_op jit(solution)/shard_map/gather | solution.py:102
  77.8 6.8 %sort.82 = (s32[8192]{0:T(1024)}, s32[8192]{0:T(1024)S(1)}) sort(s32[8192]{0:T(1024)S(1)} %broadcast_select_fusion, s32[8192]{0:T(1024)S(1)} %iota.36), dimensions={0}, to_apply=%region_4.5 | sort | flops 106496 | bytes 131072 | tf_op jit(solution)/shard_map/jit(argsort)/sort | solution.py:107
  84.6 45.5 %gather_fusion.1 = s32[8192]{0:T(1024)S(1)} fusion(s32[8192]{0:T(1024)S(1)} %broadcast_select_fusion, s32[8192]{0:T(1024)S(1)} %get-tuple-element.244), kind=kCustom, calls=%fused_computation.1 | custom fusion | bytes 98304 | tf_op jit(solution)/shard_map/gather | solution.py:108
  131.6 48.9 %gather_fusion.2 = s32[8192]{0:T(1024)S(1)} fusion(s32[65]{0:T(128)S(1)} %convert_reduce_fusion, s32[8192]{0:T(1024)S(1)} %broadcast_clamp_fusion), kind=kCustom, calls=%fused_computation.2 | custom fusion | bytes 98304 | tf_op jit(solution)/shard_map/gather | solution.py:120
  180.6 30.5 %scatter_custom_fusion = s32[4097]{0:T(1024)S(1)} fusion(s32[8192]{0:T(1024)S(1)} %bitcast.93, s32[8192]{0:T(1024)S(1)} %gather_fusion.1, s32[]{:T(128)} %constant.117.clone.1), kind=kCustom, calls=%fused_computation.106 | custom fusion | bytes 16392 | tf_op jit(solution)/shard_map/scatter | solution.py:126
  211.8 13.0 %all-to-all-start = ((s32[64,1,64]{2,1,0:T(1,128)}), s32[64,1,64]{2,1,0:T(1,128)S(1)}, u32[]{:S(2)}, u32[]{:S(2)}) async-start(s32[64,1,64]{2,1,0:T(1,128)} %all_to_all.15), calls=%async_computation | async-start | bytes 65536 | tf_op jit(solution)/shard_map/all_to_all | solution.py:138
  224.8 30.5 %scatter_custom_fusion.1 = s32[8192]{0:T(1024)S(1)} fusion(s32[8192]{0:T(1024)S(1)} %get-tuple-element.243, s32[8192]{0:T(1024)S(1)} %get-tuple-element.235, s32[]{:T(128)} %constant.67.clone.1), kind=kCustom, calls=%fused_computation.103 | custom fusion | bytes 32772 | tf_op jit(solution)/shard_map/scatter | solution.py:122
  255.3 78.7 %while.42 = (s32[]{:T(128)}, f32[4096,128]{1,0:T(8,128)S(1)}, f32[4096]{0:T(1024)S(1)}, s32[4,2048]{1,0:T(4,128)S(1)}, bf16[4,2048,128]{2,1,0:T(8,128)(2,1)}, /*index=5*/s32[]{:T(128)}, s32[]{:T(128)}) while((s32[]{:T(128)}, f32[4096,128]{1,0:T(8,128)S(1)}, f32[4096]{0:T(1024)S(1)}, s32[4,2048]{1,0:T(4,128)S(1)}, ...), condition=%wide.region_11.12_spmd.clone, body=%wide.region_9.11_spmd.clone.sunk | while | flops 2182090752 | bytes 4817500 | solution.py:83
  255.6 11.1 %fusion.69 = f32[4096,128]{1,0:T(8,128)S(1)} fusion(s32[2048]{0:T(1024)S(1)} %bitcast.87, f32[4096,128]{1,0:T(8,128)S(1)} %get-tuple-element.391, pred[]{:T(512)S(6)} %compare.53, bf16[4,2048,128]{2,1,0:T(8,128)(2,1)} %get-tuple-element.401, s32[]{:T(128)} %get-tuple-element.390), kind=kOutput, calls=%fused_computation.30.clone.1 | convolution fusion | flops 2156920832 | bytes 4727297 | tf_op jit(solution)/shard_map/while/body/eval_jaxpr/dot_general | solution.py:70
  266.7 5.3 fusion.70
  272.0 11.1 %fusion.69 = f32[4096,128]{1,0:T(8,128)S(1)} fusion(s32[2048]{0:T(1024)S(1)} %bitcast.87, f32[4096,128]{1,0:T(8,128)S(1)} %get-tuple-element.391, pred[]{:T(512)S(6)} %compare.53, bf16[4,2048,128]{2,1,0:T(8,128)(2,1)} %get-tuple-element.401, s32[]{:T(128)} %get-tuple-element.390), kind=kOutput, calls=%fused_computation.30.clone.1 | convolution fusion | flops 2156920832 | bytes 4727297 | tf_op jit(solution)/shard_map/while/body/eval_jaxpr/dot_general | solution.py:70
  283.1 5.3 fusion.70
  288.4 11.1 %fusion.69 = f32[4096,128]{1,0:T(8,128)S(1)} fusion(s32[2048]{0:T(1024)S(1)} %bitcast.87, f32[4096,128]{1,0:T(8,128)S(1)} %get-tuple-element.391, pred[]{:T(512)S(6)} %compare.53, bf16[4,2048,128]{2,1,0:T(8,128)(2,1)} %get-tuple-element.401, s32[]{:T(128)} %get-tuple-element.390), kind=kOutput, calls=%fused_computation.30.clone.1 | convolution fusion | flops 2156920832 | bytes 4727297 | tf_op jit(solution)/shard_map/while/body/eval_jaxpr/dot_general | solution.py:70
  299.5 5.3 fusion.70
  304.9 11.1 %fusion.69 = f32[4096,128]{1,0:T(8,128)S(1)} fusion(s32[2048]{0:T(1024)S(1)} %bitcast.87, f32[4096,128]{1,0:T(8,128)S(1)} %get-tuple-element.391, pred[]{:T(512)S(6)} %compare.53, bf16[4,2048,128]{2,1,0:T(8,128)(2,1)} %get-tuple-element.401, s32[]{:T(128)} %get-tuple-element.390), kind=kOutput, calls=%fused_computation.30.clone.1 | convolution fusion | flops 2156920832 | bytes 4727297 | tf_op jit(solution)/shard_map/while/body/eval_jaxpr/dot_general | solution.py:70
  315.9 5.3 fusion.70
  334.1 1.3 copy-done.2
  335.4 1.9 reshape_reshape.24
  337.4 3.9 pad_maximum_fusion
  341.3 10.5 %all-to-all-start.1 = ((f32[64,64,129]{2,1,0:T(8,128)}), f32[64,64,129]{2,1,0:T(8,128)}, u32[]{:S(2)}, u32[]{:S(2)}) async-start(f32[64,64,129]{2,1,0:T(8,128)} %pad_maximum_fusion), calls=%async_computation.1 | async-start | bytes 8388608 | tf_op jit(solution)/shard_map/all_to_all | solution.py:13
  354.3 94.1 %all-to-all-done.1 = f32[64,64,129]{2,1,0:T(8,128)} async-done(((f32[64,64,129]{2,1,0:T(8,128)}), f32[64,64,129]{2,1,0:T(8,128)}, u32[]{:S(2)}, u32[]{:S(2)}) %all-to-all-start.1) | async-done | bytes 2113568 | tf_op jit(solution)/shard_map/all_to_all | solution.py:13
  448.5 2.2 slice_reduce_fusion
  450.8 1.7 slice.58
  452.5 32.8 %while.43 = (s32[]{:T(128)}, f32[2048,128]{1,0:T(8,128)S(1)}, f32[2048]{0:T(1024)S(1)}, s32[2,2048]{1,0:T(2,128)S(1)}, f32[2,2048,128]{2,1,0:T(8,128)S(1)}, /*index=5*/f32[2,2048]{1,0:T(2,128)S(1)}, s32[]{:T(128)}, s32[]{:T(128)}) while((s32[]{:T(128)}, f32[2048,128]{1,0:T(8,128)S(1)}, f32[2048]{0:T(1024)S(1)}, ...), condition=%wide.region_15.16_spmd.clone, body=%wide.region_13.15_spmd.clone.sunk | while | flops 6459754496 | bytes 3235948 | solution.py:83
  452.5 13.8 %fusion.72 = f32[2048,128]{1,0:T(8,128)S(1)} fusion(s32[2048]{0:T(1024)S(1)} %bitcast.85, f32[2048,128]{1,0:T(8,128)S(1)} %get-tuple-element.413, f32[2,2048,128]{2,1,0:T(8,128)S(1)} %get-tuple-element.424, s32[]{:T(128)} %get-tuple-element.412, pred[]{:T(512)S(6)} %compare.54), kind=kOutput, calls=%fused_computation.41.clone.1 | convolution fusion | flops 6447169536 | bytes 3153925 | tf_op jit(solution)/shard_map/while/body/eval_jaxpr/dot_general | solution.py:62
  466.3 2.4 fusion.73
  468.8 13.8 %fusion.72 = f32[2048,128]{1,0:T(8,128)S(1)} fusion(s32[2048]{0:T(1024)S(1)} %bitcast.85, f32[2048,128]{1,0:T(8,128)S(1)} %get-tuple-element.413, f32[2,2048,128]{2,1,0:T(8,128)S(1)} %get-tuple-element.424, s32[]{:T(128)} %get-tuple-element.412, pred[]{:T(512)S(6)} %compare.54), kind=kOutput, calls=%fused_computation.41.clone.1 | convolution fusion | flops 6447169536 | bytes 3153925 | tf_op jit(solution)/shard_map/while/body/eval_jaxpr/dot_general | solution.py:62
  482.6 2.4 fusion.73
  486.3 1.4 maximum_bitcast_fusion
  487.7 2.1 copy.36
  489.8 4.2 all-to-all-start.2
  494.8 3.8 sort.85
  498.5 3.8 sort.86
  502.3 76.3 %all-reduce.1 = f32[512]{0:T(512)S(1)} all-reduce(f32[512]{0:T(512)S(1)} %get-tuple-element.129), channel_id=3, replica_groups=mesh['gx'=64,'gy'=4] {'gx','gy'}, use_global_device_ids=true, to_apply=%region_22.23.clone | all-reduce | flops 512 | bytes 4096
  579.4 3.8 sort.84
  585.7 3.5 gather_fusion.4
  590.2 5.4 all-to-all-start.3
  596.3 26.3 %all-reduce.4.cloned.1.call-done = f32[512,128]{1,0:T(8,128)} async-done(((f32[512,128]{1,0:T(8,128)}), f32[512,128]{1,0:T(8,128)}) %all-reduce.4.cloned.1.call-update) | async-done | bytes 262160
  625.4 3.5 gather_fusion.6
  (115 shorter events, 22.3 us)
Async XLA Ops:
  9.6 22.6 %copy-start = (s32[131072]{0:T(1024)S(1)}, s32[131072]{0:T(1024)}, u32[]{:S(2)}) copy-start(s32[131072]{0:T(1024)} %param.15) | copy-start | bytes 1572868
  32.2 45.6 %copy-start.4 = (f32[512,128]{1,0:T(8,128)}, f32[512,128]{1,0:T(8,128)S(1)}, u32[]{:S(2)}) copy-start(f32[512,128]{1,0:T(8,128)S(1)} %get-tuple-element.128) | copy-start | bytes 786436
  211.8 129.5 %all-to-all-start = ((s32[64,1,64]{2,1,0:T(1,128)}), s32[64,1,64]{2,1,0:T(1,128)S(1)}, u32[]{:S(2)}, u32[]{:S(2)}) async-start(s32[64,1,64]{2,1,0:T(1,128)} %all_to_all.15), calls=%async_computation | async-start | bytes 65536 | tf_op jit(solution)/shard_map/all_to_all | solution.py:138
  334.1 1.3 copy-start.2
  341.3 107.1 %all-to-all-start.1 = ((f32[64,64,129]{2,1,0:T(8,128)}), f32[64,64,129]{2,1,0:T(8,128)}, u32[]{:S(2)}, u32[]{:S(2)}) async-start(f32[64,64,129]{2,1,0:T(8,128)} %pad_maximum_fusion), calls=%async_computation.1 | async-start | bytes 8388608 | tf_op jit(solution)/shard_map/all_to_all | solution.py:13
  351.8 226.8 %sort.88.cloned.1.call-start = ((), (), s32[]{:S(2)}) async-start(), calls=%async_computation.5 | async-start | bytes 3145760 | tf_op jit(solution)/shard_map/jit(argsort)/sort | solution.py:161
  352.7 269.9 %all-reduce.4.cloned.1.call-start = ((), (), s32[]{:S(2)}) async-start(), calls=%async_computation.4 | async-start | bytes 524288
  485.3 1.0 copy-start.3
  489.8 93.4 %all-to-all-start.2 = ((f32[4,1,512,129]{2,1,3,0:T(1,128)}), f32[4,1,512,129]{2,1,3,0:T(1,128)S(1)}, u32[]{:S(2)}, u32[]{:S(2)}) async-start(f32[4,1,512,129]{2,1,3,0:T(1,128)} %copy.36), calls=%async_computation.2 | async-start | bytes 2113536 | tf_op jit(solution)/shard_map/all_to_all | solution.py:32
  584.2 11.5 %copy-start.5 = (bf16[512,128]{1,0:T(8,128)(2,1)S(1)}, bf16[512,128]{1,0:T(8,128)(2,1)}, u32[]{:S(2)}) copy-start(bf16[512,128]{1,0:T(8,128)(2,1)} %param.13) | copy-start | bytes 393220
  584.6 40.8 %copy-start.1 = (f32[512]{0:T(512)}, f32[512]{0:T(512)S(1)}, u32[]{:S(2)}) copy-start(f32[512]{0:T(512)S(1)} %slice_reduce_fusion.2) | copy-start | bytes 6148
  590.2 33.8 %all-to-all-start.3 = ((f32[64,8,129]{2,1,0:T(8,128)}), f32[64,8,129]{2,1,0:T(8,128)S(1)}, u32[]{:S(2)}, u32[]{:S(2)}) async-start(f32[64,8,129]{2,1,0:T(8,128)} %pad_maximum_fusion.1), calls=%async_computation.3 | async-start | bytes 1048576 | tf_op jit(solution)/shard_map/all_to_all | solution.py:13
Sparse Core Ops, SparseCore 0:
  355.8 40.8 sort.90.cloned.1.call-done
  (1 shorter events, 0.0 us)
Sparse Core Ops, SparseCore 1:
  358.7 263.9 all-reduce.3
where the time goes:
time: 650 us; the launch traced here: 638 us
  local copies, waits for them, and re-layouts  226 us (35%)
  waiting for transfers between devices  121 us (19%)
  matrix products  82.5 us (13%)
  blocking collectives  76.3 us (12%)
  other arithmetic  68.9 us (11%)
  starting transfers between devices  33.1 us (5%)
  between operations  16.3 us (3%)
  loops' own time  13.8 us (2%)
    all_to_all x2, waiting for transfers between devices, sent_together(): lax.all_to_all(both, axis, split_axis=split_dim, concat_axis=concat_dim,...  94.1 us
    unnamed x1, blocking collectives  76.3 us
    dot_general x8, matrix products, add_block(): lax.dot_general(onehot, block_values, (((0,), (0,)), ((), ())), preferred...  55 us
    gather x1, local copies, waits for them, and re-layouts, body(): before[sorted_owner]  48.9 us
    gather x1, local copies, waits for them, and re-layouts, body(): sorted_slots = sort_keys[ordering]  45.5 us
    gather x1, local copies, waits for them, and re-layouts, body(): slot_ids = key_slot[row_keys]  45.5 us
    reduce_sum x10, other arithmetic, add_block(): jnp.sum(matches.astype(jnp.float32) * block_weights[:, None], axis=0)  31.1 us
    scatter x1, local copies, waits for them, and re-layouts, body(): jnp.full((segments + 1,), -1, jnp.int32).at[segment].set(sorted_slots)  30.5 us
  transfers between devices with their start and end apart: 5, of which 2 were waited for; matrix products, arithmetic and copies ran while one was open for 26% of the time, Pallas kernels for 0%

commit v1 on v0

v1 whole, which is shorter than its diff:
```python
import functools

import jax
import jax.numpy as jnp
from jax import lax
from jax.experimental import pallas as pl
from jax.experimental.pallas import tpu as pltpu
from jax.sharding import PartitionSpec as P

MESH = pl.DeviceIdType.MESH
F32, BF16, I32, I16 = jnp.float32, jnp.bfloat16, jnp.int32, jnp.int16
LN2 = 0.6931471805599453

W = 128
GX, GY = 64, 4
KEYS = 131072
KD = 512
OWN = 2048
CAPK = 64
HG = 8
MSG = 80
LANES = 1024
VMEM = pl.BlockSpec(memory_space=pltpu.VMEM)


def iota(shape, dim):
    return lax.broadcasted_iota(I32, shape, dim)


def onehot(rows, lanes, base, labels):
    return jnp.where(iota((rows, lanes), 0) + base == labels, 1.0, 0.0).astype(BF16)


def dot(a, b):
    return jnp.dot(a, b, preferred_element_type=F32)


def dot_t(a, b):
    return lax.dot_general(a, b, (((1,), (1,)), ((), ())), preferred_element_type=F32)


def power(e):
    return jnp.exp(e * LN2)


def encode(v):
    top = jnp.max(jnp.abs(v), axis=1, keepdims=True)
    e = jnp.ceil(jnp.log(jnp.maximum(top, 1e-30)) * (1.0 / LN2) - 14.99)
    e = jnp.maximum(e, -100.0)
    q = jnp.floor(v * power(-e) + 0.5).astype(I32)
    return q, e


def gather_kernel(keys_ref, x_ref, ks_ref, hk_ref, msg_ref,
                  tab, shi_s, slo_s, seg_s, xe, pt, rk, acc, hq, hx):
    chunks = keys_ref.shape[0]
    hi_n, lo_n = ks_ref.shape
    ks = ks_ref[...]
    key_id = iota((hi_n, lo_n), 0) * lo_n + iota((hi_n, lo_n), 1)
    p1 = (ks >> 11) * 2 + ((ks >> 8) & 1)
    p1 = jnp.where(key_id == hk_ref[:, 0:1], 128, p1)
    p1 = jnp.where(key_id == hk_ref[:, 1:2], 129, p1)
    p2 = ks & 255
    tab[0:lo_n, :] = p1.astype(F32).T.astype(BF16)
    tab[lo_n : 2 * lo_n, :] = p2.astype(F32).T.astype(BF16)
    pt[...] = jnp.zeros_like(pt)

    def look(c, carry):
        key = keys_ref[pl.ds(c, 1), :]
        hi, lo = key >> 8, key & 255
        t = dot(tab[...], onehot(hi_n, LANES, 0, hi))
        mine = iota((lo_n, LANES), 0) == lo
        a = jnp.sum(jnp.where(mine, t[:lo_n], 0.0), axis=0, keepdims=True).astype(I32)
        b = jnp.sum(jnp.where(mine, t[lo_n:], 0.0), axis=0, keepdims=True).astype(I32)
        heavy = a >= 128
        shi = jnp.where(heavy, -1, (a >> 1) * 8 + ((key >> 9) & 3) * 2 + (a & 1))
        shi_s[pl.ds(c, 1), :] = shi
        slo_s[pl.ds(c, 1), :] = b
        seg_s[pl.ds(c, 1), :] = jnp.where(
            heavy, GX * CAPK + (key >> 9) * 2 + (a - 128), (a >> 1) * CAPK
        )
        pt[...] += dot_t(onehot(lo_n, LANES, 0, b), onehot(hi_n, LANES, 0, shi))
        return carry

    lax.fori_loop(0, chunks, look, 0)

    here = jnp.where(pt[...] > 0.5, 1.0, 0.0).astype(BF16)
    lower = jnp.where(iota((lo_n, lo_n), 1) < iota((lo_n, lo_n), 0), 1.0, 0.0).astype(BF16)
    r0, r1 = iota((hi_n, hi_n), 0), iota((hi_n, hi_n), 1)
    before = jnp.where((r0 < r1) & ((r0 >> 3) == (r1 >> 3)), 1.0, 0.0).astype(BF16)
    column = dot(jnp.ones((lo_n, lo_n), BF16), here).astype(BF16)
    rk[...] = (dot(lower, here) + dot(column, before)).astype(BF16)

    def rank(c, carry):
        shi = shi_s[pl.ds(c, 1), :]
        slo = slo_s[pl.ds(c, 1), :]
        t = dot(rk[...], onehot(hi_n, LANES, 0, shi))
        mine = iota((lo_n, LANES), 0) == slo
        r = jnp.sum(jnp.where(mine, t, 0.0), axis=0, keepdims=True).astype(I32)
        seg_s[pl.ds(c, 1), :] = seg_s[pl.ds(c, 1), :] + jnp.where(shi < 0, 0, r)
        line = iota((W, LANES), 0)
        ext = jnp.where(line == 0, 1, jnp.where(line == 1, slo, jnp.where(line == 2, shi & 7, 0)))
        at = pl.ds(pl.multiple_of(c * LANES, LANES), LANES)
        xe[at, 0:W] = x_ref[at, :]
        xe[at, W : 2 * W] = ext.astype(F32).T.astype(BF16)
        return carry

    lax.fori_loop(0, chunks, rank, 0)

    def sums(base):
        acc[...] = jnp.zeros_like(acc)

        def step(c, carry):
            at = pl.ds(pl.multiple_of(c * LANES, LANES), LANES)
            acc[...] += dot(onehot(512, LANES, base, seg_s[pl.ds(c, 1), :]), xe[at, :])
            return carry

        lax.fori_loop(0, chunks, step, 0)
        return acc[:, 0:W], acc[:, W : 2 * W]

    lane = iota((512, W), 1)
    v, ext = sums(GX * CAPK)
    q, e = encode(v)
    hq[...] = q
    hx[...] = jnp.where(lane == 64, ext[:, 0:1], jnp.where(lane == 65, e, 0.0)).astype(I32)

    def owners(m, carry):
        v, ext = sums(m * 512)
        q, e = encode(v)
        t = jnp.where(lane == 3, e, ext).T[0:8]
        cnt = t[0:1]
        slot = jnp.where(
            cnt > 0.5, jnp.floor((t[1:2] + 256.0 * t[2:3]) / jnp.maximum(cnt, 1.0) + 0.5), -1.0
        )
        line = iota((8, 512), 0)
        meta = jnp.where(line == 0, slot, jnp.where(line == 1, cnt, t[3:4])).astype(I32)
        for i in range(8):
            o = m * 8 + i
            part = meta[:, (i // 2) * W : (i // 2 + 1) * W]
            if i % 2:
                part = pltpu.roll(part, 64, 1)
            at = pl.ds(pl.multiple_of(o * 8, 8), 8)
            part = jnp.where(iota((8, W), 1) < 64, part, hx[at, :])
            msg_ref[pl.ds(o, 1), 0:64, :] = q[i * 64 : (i + 1) * 64].astype(I16)[None]
            tail = jnp.concatenate([hq[at, :], part], axis=0)
            msg_ref[pl.ds(o, 1), 64:80, :] = tail.astype(I16)[None]
        return carry

    lax.fori_loop(0, GX // 8, owners, 0)


def gather(keys, x, ks, hk):
    rows = x.shape[0]
    chunks = rows // LANES
    return pl.pallas_call(
        gather_kernel,
        out_shape=jax.ShapeDtypeStruct((GX, MSG, W), I16),
        in_specs=[VMEM] * 4,
        out_specs=VMEM,
        scratch_shapes=[
            pltpu.VMEM((512, 512), BF16),
            pltpu.VMEM((chunks, LANES), I32),
            pltpu.VMEM((chunks, LANES), I32),
            pltpu.VMEM((chunks, LANES), I32),
            pltpu.VMEM((rows, 2 * W), BF16),
            pltpu.VMEM((256, 512), F32),
            pltpu.VMEM((256, 512), BF16),
            pltpu.VMEM((512, 2 * W), F32),
            pltpu.VMEM((512, W), I32),
            pltpu.VMEM((512, W), I32),
        ],
        compiler_params=pltpu.CompilerParams(vmem_limit_bytes=50 * 2**20),
        name="gather_rows",
    )(keys, x, ks, hk)


def peer_gx(me, k):
    core, z, x = me % 2, (me // 2) % 8, me // 16
    j = k // 2
    zi, dx = j // 4, j % 4
    dz = ((zi + 1) // 2) * (1 - 2 * ((zi + 1) % 2))
    return (((x + dx) % 4) * 8 + (z + 8 + dz) % 8) * 2 + (core + k) % 2


def source_gx(me, k):
    core, z, x = me % 2, (me // 2) % 8, me // 16
    j = k // 2
    zi, dx = j // 4, j % 4
    dz = ((zi + 1) // 2) * (1 - 2 * ((zi + 1) % 2))
    return (((x + 4 - dx) % 4) * 8 + (z + 8 - dz) % 8) * 2 + (core + k) % 2


def peer_ring(n, me, k):
    return (me + k) % n


def source_ring(n, me, k):
    return (me + n - k) % n


def exchange_kernel(axis, n, to, frm, x_ref, o_ref, ssem, rsem, lsem):
    me = lax.axis_index(axis)
    barrier = pltpu.get_barrier_semaphore()

    def greet(k, carry):
        pl.semaphore_signal(barrier, inc=1, device_id={axis: to(me, k)}, device_id_type=MESH)
        return carry

    lax.fori_loop(1, n, greet, 0)
    own = pltpu.make_async_copy(x_ref.at[me], o_ref.at[me], lsem)
    own.start()
    pl.semaphore_wait(barrier, n - 1)

    def send(k, carry):
        p = to(me, k)
        pltpu.make_async_remote_copy(
            src_ref=x_ref.at[p], dst_ref=o_ref.at[me], send_sem=ssem.at[p], recv_sem=rsem.at[me],
            device_id={axis: p}, device_id_type=MESH,
        ).start()
        return carry

    lax.fori_loop(1, n, send, 0)
    own.wait()

    def finish(k, carry):
        p, s = to(me, k), frm(me, k)
        pltpu.make_async_remote_copy(
            src_ref=x_ref.at[p], dst_ref=o_ref.at[s], send_sem=ssem.at[p], recv_sem=rsem.at[s],
            device_id={axis: p}, device_id_type=MESH,
        ).wait()
        return carry

    lax.fori_loop(1, n, finish, 0)


def exchange(x, axis, n, to, frm, cid):
    return pl.pallas_call(
        functools.partial(exchange_kernel, axis, n, to, frm),
        out_shape=jax.ShapeDtypeStruct(x.shape, x.dtype),
        in_specs=[VMEM],
        out_specs=VMEM,
        scratch_shapes=[
            pltpu.SemaphoreType.DMA((n,)),
            pltpu.SemaphoreType.DMA((n,)),
            pltpu.SemaphoreType.DMA,
        ],
        compiler_params=pltpu.CompilerParams(
            collective_id=cid, has_side_effects=True, vmem_limit_bytes=32 * 2**20
        ),
        name="exchange_" + axis + str(cid),
    )(x)


def slots_of(ks, me):
    mine = jnp.where((ks >> 11) == me, 1.0, 0.0)
    upper = jnp.where(iota((KD, KD), 0) < iota((KD, KD), 1), 1.0, 0.0).astype(BF16)
    w = dot(mine.astype(BF16), upper)
    pos = (ks & (KD - 1)).astype(F32)
    lane = iota((GX, W), 1)
    table = jnp.zeros((GX, W), F32)
    for k in range(8):
        s = jnp.sum(jnp.where((mine > 0.5) & (w == float(k)), pos, 0.0), axis=1, keepdims=True)
        table = jnp.where(lane == k, s, table)
    high = jnp.floor(table * (1.0 / 256.0))
    low = table - 256.0 * high
    repeat = jnp.where((iota((KD, GX), 0) >> 3) == iota((KD, GX), 1), 1.0, 0.0).astype(BF16)
    each = 256.0 * dot(repeat, high.astype(BF16)) + dot(repeat, low.astype(BF16))
    pick = iota((KD, W), 1) == (iota((KD, W), 0) & 7)
    return jnp.sum(jnp.where(pick, each, 0.0), axis=1, keepdims=True).astype(I32)


def owner_kernel(msg_ref, ks_ref, out_ref, v_s, meta_s, scol, acc, tal, heavy, hcount):
    me = lax.axis_index("gx")
    for q in range(GY):
        scol[q * KD : (q + 1) * KD, :] = slots_of(ks_ref[:, q * KD : (q + 1) * KD], me) + q * KD
    heavy[...] = jnp.zeros_like(heavy)
    hcount[...] = jnp.zeros_like(hcount)
    lane = iota((8, W), 1)

    def unpack(p, carry):
        metas = []
        for i in range(2):
            s = 2 * p + i
            q = msg_ref[pl.ds(s, 1), 0:64, :][0].astype(I32)
            at = pl.ds(pl.multiple_of(s * 64, 64), 64)
            high = q >> 8
            v_s[at, 0:W] = high.astype(F32).astype(BF16)
            v_s[at, W : 2 * W] = (q - high * 256).astype(F32).astype(BF16)
            tail = msg_ref[pl.ds(s, 1), 64:80, :][0].astype(I32)
            meta = tail[8:16]
            heavy[...] += tail[0:8].astype(F32) * power(meta[:, 65:66].astype(F32))
            hcount[...] += meta[:, 64:65].astype(F32) + jnp.zeros((8, W), F32)
            metas.append(meta)
        both = jnp.where(lane < 64, metas[0], pltpu.roll(metas[1], 64, 1))
        meta_s[:, pl.ds(pl.multiple_of(p * W, W), W)] = both
        return carry

    lax.fori_loop(0, GX // 2, unpack, 0)

    def quarter(q, carry):
        acc[...] = jnp.zeros_like(acc)
        tal[...] = jnp.zeros_like(tal)
        labels = scol[pl.ds(pl.multiple_of(q * KD, KD), KD), :]

        def step(c, carry):
            at = pl.ds(pl.multiple_of(c * LANES, LANES), LANES)
            meta = meta_s[:, at]
            mine = labels == meta[0:1]
            scale = power(meta[2:3].astype(F32))
            oh = jnp.where(mine, scale, 0.0).astype(BF16)
            acc[...] += dot(oh, v_s[at, :])
            hits = jnp.where(mine, meta[1:2].astype(F32), 0.0)
            t = hits[:, 0:W]
            for i in range(1, LANES // W):
                t = t + hits[:, i * W : (i + 1) * W]
            tal[...] += t
            return carry

        lax.fori_loop(0, GX * CAPK // LANES, step, 0)
        out_ref[pl.ds(q, 1), 0:KD, :] = (acc[:, 0:W] * 256.0 + acc[:, W : 2 * W])[None]
        t = jnp.sum(tal[...].T, axis=0, keepdims=True)
        line = iota((8, W), 0)
        rows = jnp.zeros((8, W), F32)
        for i in range(4):
            rows = jnp.where(line == i, t[:, i * W : (i + 1) * W], rows)
        out_ref[pl.ds(q, 1), KD : KD + 8, :] = rows[None]
        return carry

    lax.fori_loop(0, GY, quarter, 0)
    line = iota((8, W), 0)
    for q in range(GY):
        rows = jnp.where(line == 0, heavy[2 * q : 2 * q + 1], 0.0)
        rows = jnp.where(line == 1, heavy[2 * q + 1 : 2 * q + 2], rows)
        rows = jnp.where(line == 2, hcount[2 * q : 2 * q + 1], rows)
        rows = jnp.where(line == 3, hcount[2 * q + 1 : 2 * q + 2], rows)
        out_ref[q, KD + 8 : KD + 16, :] = rows


def owner(msg, ks):
    return pl.pallas_call(
        owner_kernel,
        out_shape=jax.ShapeDtypeStruct((GY, KD + 16, W), F32),
        in_specs=[VMEM] * 2,
        out_specs=VMEM,
        scratch_shapes=[
            pltpu.VMEM((GX * CAPK, 2 * W), BF16),
            pltpu.VMEM((8, GX * CAPK), I32),
            pltpu.VMEM((OWN, 1), I32),
            pltpu.VMEM((KD, 2 * W), F32),
            pltpu.VMEM((KD, W), F32),
            pltpu.VMEM((8, W), F32),
            pltpu.VMEM((8, W), F32),
        ],
        compiler_params=pltpu.CompilerParams(vmem_limit_bytes=50 * 2**20),
        name="owner_sums",
    )(msg, ks)


def quarter_kernel(got_ref, ks_ref, out_ref, slots_ref, heavy_ref):
    me = lax.axis_index("gx")
    total = got_ref[0] + got_ref[1] + got_ref[2] + got_ref[3]
    counts = total[KD : KD + 8]
    square = jnp.concatenate([counts, jnp.zeros((W - 8, W), F32)], axis=0).T
    column = jnp.concatenate([square[:, i : i + 1] for i in range(4)], axis=0)
    out_ref[...] = total[0:KD] * lax.rsqrt(1.0 + column)
    pos = slots_of(ks_ref[...], me)
    slots_ref[...] = jnp.sum(
        jnp.where(pos == iota((KD, KD), 1), column, 0.0), axis=0, keepdims=True
    )
    tail = total[KD + 8 : KD + 16]
    heavy_ref[...] = tail * lax.rsqrt(1.0 + pltpu.roll(tail, 6, 0))


def quarter(got, ks):
    return pl.pallas_call(
        quarter_kernel,
        out_shape=(
            jax.ShapeDtypeStruct((KD, W), F32),
            jax.ShapeDtypeStruct((1, KD), F32),
            jax.ShapeDtypeStruct((8, W), F32),
        ),
        in_specs=[VMEM] * 2,
        out_specs=(VMEM,) * 3,
        compiler_params=pltpu.CompilerParams(vmem_limit_bytes=32 * 2**20),
        name="quarter_totals",
    )(got, ks)


def result_kernel(got_ref, orders_ref, row_ref, col_ref, hloc_ref, heavy_ref, out_ref, report_ref):
    own_row = row_ref[...] >> 11
    own_col = col_ref[...] >> 11
    j0, j1 = iota((KD, KD), 0), iota((KD, KD), 1)
    w = jnp.sum(jnp.where((own_row == own_col) & (j1 < j0), 1.0, 0.0), axis=1, keepdims=True)
    place = own_col * 8 + w.astype(I32)
    oh = jnp.where(place == j1, 1.0, 0.0).astype(BF16)
    got = got_ref[...]
    high = got.astype(BF16)
    low = (got - high.astype(F32)).astype(BF16)
    total = dot(oh, high) + dot(oh, low)
    orders = orders_ref[...].astype(F32)
    line = iota((KD, W), 0)
    reports = []
    for h in range(2):
        here = line == hloc_ref[h]
        total = jnp.where(here, heavy_ref[h : h + 1, :], total)
        mine = jnp.sum(jnp.where(here, orders, 0.0), axis=0, keepdims=True)
        reports.append(mine * heavy_ref[h : h + 1, :])
    out_ref[...] = (orders * total).astype(BF16)
    report_ref[...] = jnp.concatenate(reports, axis=0).astype(BF16)


def outputs(got, orders, row, col, hloc, heavy):
    return pl.pallas_call(
        result_kernel,
        out_shape=(jax.ShapeDtypeStruct((KD, W), BF16), jax.ShapeDtypeStruct((2, W), BF16)),
        in_specs=[VMEM, VMEM, VMEM, VMEM, pl.BlockSpec(memory_space=pltpu.SMEM), VMEM],
        out_specs=(VMEM, VMEM),
        compiler_params=pltpu.CompilerParams(vmem_limit_bytes=32 * 2**20),
        name="range_outputs",
    )(got, orders, row, col, hloc, heavy)


def body(measures, row_keys, orders, heavy_keys, key_slot):
    index_x, index_y = lax.axis_index("gx"), lax.axis_index("gy")
    device = index_x * GY + index_y
    rows = measures.shape[0]
    keys = row_keys.reshape(rows // LANES, LANES)
    pairs = jnp.repeat(heavy_keys.reshape(-1, 2), 2, axis=0)
    messages = gather(keys, measures, key_slot.reshape(KEYS // 256, 256), pairs)
    arrived = exchange(messages, "gx", GX, peer_gx, source_gx, 0)
    blocks = key_slot.reshape(GX, GY * KD)
    dense = owner(arrived, blocks)
    ring = functools.partial(peer_ring, GY), functools.partial(source_ring, GY)
    quarters = exchange(dense, "gy", GY, *ring, 1)
    own_blocks = lax.dynamic_slice_in_dim(blocks, index_y * KD, KD, axis=1)
    scaled, slot_rows, heavy = quarter(quarters, own_blocks)
    moved = exchange(scaled.reshape(GX, 8, W), "gx", GX, peer_gx, source_gx, 2)
    own_slots = lax.dynamic_slice_in_dim(key_slot, device * KD, KD)
    heavy_local = lax.dynamic_slice_in_dim(heavy_keys, device * 2, 2) - device * KD
    result, report = outputs(
        moved.reshape(KD, W), orders, own_slots.reshape(1, KD), own_slots.reshape(KD, 1),
        heavy_local, heavy,
    )
    return (result, report, slot_rows.reshape(KD))


def solution(mesh):
    return jax.shard_map(
        body,
        mesh=mesh,
        in_specs=(P(("gx", "gy"), None), P(("gx", "gy")), P(("gx", "gy"), None), P(), P()),
        out_specs=(P(("gx", "gy"), None), P(("gx", "gy"), None), P(("gx", "gy"))),
        check_vma=False,
    )
```

time: 650 us -> 157 us (0.24); the launches traced: 638 us -> 156 us
  local copies, waits for them, and re-layouts: 226 us -> 3.22 us
  Pallas kernels: 0 us -> 152 us
  waiting for transfers between devices: 121 us -> 0 us
  matrix products: 82.5 us -> 0 us
  blocking collectives: 76.3 us -> 0 us
  other arithmetic: 68.9 us -> 0.76 us
  starting transfers between devices: 33.1 us -> 0 us
  between operations: 16.3 us -> 0.73 us
  loops' own time: 13.8 us -> 0 us
    pallas_call x0 -> x7, Pallas kernels: none -> 152 us  [the longest x3 80.9 us: exchange(): pl.pallas_call(functools.partial(exchange_kernel, axis, n, to, frm), out_...]
    gather x8 -> x0, local copies, waits for them, and re-layouts: 150 us -> none  [the longest x1 48.9 us: body(): before[sorted_owner]]
    all_to_all x4 -> x0, waiting for transfers between devices: 94.1 us -> none  [the longest x2 94.1 us: sent_together(): lax.all_to_all(both, axis, split_axis=split_dim, concat_axis=concat_dim,...]
    dot_general x10 -> x0, matrix products: 82.5 us -> none  [the longest x8 55 us: add_block(): lax.dot_general(onehot, block_values, (((0,), (0,)), ((), ())), preferred...]
    unnamed x1 -> x0, blocking collectives: 76.3 us -> none
    scatter x2 -> x0, local copies, waits for them, and re-layouts: 61 us -> none  [the longest x1 30.5 us: body(): jnp.full((segments + 1,), -1, jnp.int32).at[segment].set(sorted_slots)]
    all_to_all x4 -> x0, starting transfers between devices: 33.1 us -> none  [the longest x2 15.9 us: sent_together(): lax.all_to_all(both, axis, split_axis=split_dim, concat_axis=concat_dim,...]
    reduce_sum x13 -> x0, other arithmetic: 32.8 us -> none  [the longest x10 31.1 us: add_block(): jnp.sum(matches.astype(jnp.float32) * block_weights[:, None], axis=0)]
  transfers between devices with their start and end apart: 5 -> 0, of which waited for: 2 -> 0; matrix products, arithmetic and copies ran while one was open for 26% -> 0% of each run, Pallas kernels for 0% -> 0%
where the time goes in v1:
time: 157 us; the launch traced here: 156 us
  Pallas kernels  152 us (97%)
  local copies, waits for them, and re-layouts  3.22 us (2%)
    pallas_call x3, Pallas kernels, exchange(): pl.pallas_call(functools.partial(exchange_kernel, axis, n, to, frm), out_...  80.9 us
    pallas_call x1, Pallas kernels, gather(): pl.pallas_call(gather_kernel, out_shape=jax.ShapeDtypeStruct((GX, MSG, W)...  52.3 us
    pallas_call x1, Pallas kernels, owner(): pl.pallas_call(owner_kernel, out_shape=jax.ShapeDtypeStruct((GY, KD + 16,...  14.7 us

profile of v1, /device:TPU:1, one launch (start us, length us, event | category | flops | bytes accessed | tf_op | source)
XLA Modules:
  0.0 156.3 jit_solution(4416452051823595669)
XLA Ops:
  0.6 0.8 reshape.36.keys_ref
  1.4 1.2 reshape.37.ks_ref
  2.6 0.8 reshape.38
  3.4 0.1 broadcast_in_dim.3
  3.5 52.3 %gather_rows.1.x_ref = s16[64,80,128]{2,1,0:T(8,128)(2,1)S(1)} custom-call(s32[8,1024]{1,0:T(8,128)S(1)} %reshape.36.keys_ref, bf16[8192,128]{1,0:T(8,128)(2,1)} %x_ref.1, s32[512,256]{1,0:T(8,128)S(1)} %reshape.37.ks_ref, s32[512,2]{1,0:T(8,128)S(1)} %bitcast.6), custom_call_target="tpu_custom_call" | custom-call | tf_op jit(solution)/shard_map/gather_rows/pallas_call | solution.py:155
  55.8 0.0 copy-start.1
  55.8 44.2 %exchange_gx0.1.msg_ref = s16[64,80,128]{2,1,0:T(8,128)(2,1)S(1)} custom-call(s16[64,80,128]{2,1,0:T(8,128)(2,1)S(1)} %gather_rows.1.x_ref), custom_call_target="tpu_custom_call" | custom-call | tf_op jit(solution)/shard_map/exchange_gx0/pallas_call | solution.py:237
  100.1 0.0 copy-done.1
  100.1 0.1 reshape.40.ks_ref
  100.2 14.7 %owner_sums.1.x_ref = f32[4,528,128]{2,1,0:T(8,128)S(1)} custom-call(s16[64,80,128]{2,1,0:T(8,128)(2,1)S(1)} %exchange_gx0.1.msg_ref, s32[64,2048]{1,0:T(8,128)S(1)} %reshape.40.ks_ref), custom_call_target="tpu_custom_call" | custom-call | tf_op jit(solution)/shard_map/owner_sums/pallas_call | solution.py:340
  114.9 16.2 %exchange_gy1.1.got_ref = f32[4,528,128]{2,1,0:T(8,128)S(1)} custom-call(f32[4,528,128]{2,1,0:T(8,128)S(1)} %owner_sums.1.x_ref), custom_call_target="tpu_custom_call" | custom-call | tf_op jit(solution)/shard_map/exchange_gy1/pallas_call | solution.py:237
  131.0 0.0 copy-start
  131.1 1.4 quarter_totals.1
  132.5 20.6 %exchange_gx2.1 = f32[64,8,128]{2,1,0:T(8,128)S(1)} custom-call(f32[64,8,128]{2,1,0:T(8,128)S(1)} %bitcast.8), custom_call_target="tpu_custom_call" | custom-call | tf_op jit(solution)/shard_map/exchange_gx2/pallas_call | solution.py:237
  153.1 0.1 dynamic_slice.10
  153.2 0.1 copy.8.col_ref
  153.3 0.8 dynamic-slice_subtract_fusion.hloc_ref
  154.1 0.0 copy-done
  154.1 2.2 %range_outputs.1 = (bf16[512,128]{1,0:T(8,128)(2,1)}, bf16[2,128]{1,0:T(2,128)(2,1)}) custom-call(f32[512,128]{1,0:T(8,128)S(1)} %bitcast.7, bf16[512,128]{1,0:T(8,128)(2,1)S(1)} %copy-done, s32[1,512]{1,0:T(1,128)S(1)} %bitcast.10, s32[512,1]{1,0:T(8,128)S(1)} %copy.8.col_ref, s32[2]{0:T(128)S(1)} %dynamic-slice_subtract_fusion.hloc_ref, ...), custom_call_target="tpu_custom_call" | custom-call | tf_op jit(solution)/shard_map/range_outputs/pallas_call | solution.py:413
  (1 shorter events, 0.0 us)
Async XLA Ops:
  55.8 44.2 %copy-start.1 = (s32[131072]{0:T(1024)S(1)}, s32[131072]{0:T(1024)}, u32[]{:S(2)}) copy-start(s32[131072]{0:T(1024)} %param.9) | copy-start | bytes 1572868
  131.0 23.1 %copy-start = (bf16[512,128]{1,0:T(8,128)(2,1)S(1)}, bf16[512,128]{1,0:T(8,128)(2,1)}, u32[]{:S(2)}) copy-start(bf16[512,128]{1,0:T(8,128)(2,1)} %orders_ref.1) | copy-start | bytes 393220

commit v2 on v1

v2 whole, which is shorter than its diff:
```python
import jax
import jax.numpy as jnp
from jax import lax
from jax.experimental import pallas as pl
from jax.experimental.pallas import tpu as pltpu
from jax.sharding import PartitionSpec as P

MESH = pl.DeviceIdType.MESH
F32, BF16, I32, I16 = jnp.float32, jnp.bfloat16, jnp.int32, jnp.int16
LN2 = 0.6931471805599453

W = 128
GX, GY = 64, 4
KEYS = 131072
KD = 512
OWN = 2048
CAPK = 64
HG = 8
MSG = 80
LANES = 1024
VMEM = pl.BlockSpec(memory_space=pltpu.VMEM)


def iota(shape, dim):
    return lax.broadcasted_iota(I32, shape, dim)


def onehot(rows, lanes, base, labels):
    labels = (labels - base).astype(I16)
    return jnp.where(iota((rows, lanes), 0).astype(I16) == labels, jnp.ones((), BF16), jnp.zeros((), BF16))


def dot(a, b):
    return jnp.dot(a, b, preferred_element_type=F32)


def dot_t(a, b):
    return lax.dot_general(a, b, (((1,), (1,)), ((), ())), preferred_element_type=F32)


def power(e):
    return jnp.exp(e * LN2)


def encode(v):
    top = jnp.max(jnp.abs(v), axis=1, keepdims=True)
    e = jnp.ceil(jnp.log(jnp.maximum(top, 1e-30)) * (1.0 / LN2) - 14.99)
    e = jnp.maximum(e, -100.0)
    q = jnp.floor(v * power(-e) + 0.5).astype(I32)
    return q, e


def slots_of(ks, me):
    mine = jnp.where((ks >> 11) == me, 1.0, 0.0)
    upper = jnp.where(iota((KD, KD), 0) < iota((KD, KD), 1), 1.0, 0.0).astype(BF16)
    w = dot(mine.astype(BF16), upper)
    pos = (ks & (KD - 1)).astype(F32)
    lane = iota((GX, W), 1)
    table = jnp.zeros((GX, W), F32)
    for k in range(8):
        s = jnp.sum(jnp.where((mine > 0.5) & (w == float(k)), pos, 0.0), axis=1, keepdims=True)
        table = jnp.where(lane == k, s, table)
    high = jnp.floor(table * (1.0 / 256.0))
    low = table - 256.0 * high
    repeat = jnp.where((iota((KD, GX), 0) >> 3) == iota((KD, GX), 1), 1.0, 0.0).astype(BF16)
    each = 256.0 * dot(repeat, high.astype(BF16)) + dot(repeat, low.astype(BF16))
    pick = iota((KD, W), 1) == (iota((KD, W), 0) & 7)
    return jnp.sum(jnp.where(pick, each, 0.0), axis=1, keepdims=True).astype(I32)


def offset(m):
    zi = 7 - m
    return ((zi + 1) // 2) * (1 - 2 * ((zi + 1) % 2))


def pair_at(me, dx, dz):
    z, x = (me // 2) % 8, me // 16
    return (((x + 4 + dx) % 4) * 8 + (z + 8 + dz) % 8) * 2


def join_kernel(keys_ref, x_ref, ks_ref, hk_ref, blocks_ref,
                moved_ref, slots_ref, heavy_ref,
                tab, shi_s, slo_s, seg_s, xe, pt, rk, acc, hq, hx, msg, arr,
                v_s, meta_s, scol, dense, tal, hsum, hcount, quarters, parts, scaled,
                ssem, rsem, ysend, yrecv, fsend, frecv):
    gx, gy = lax.axis_index("gx"), lax.axis_index("gy")
    barrier = pltpu.get_barrier_semaphore()

    def greet(k, carry):
        pl.semaphore_signal(barrier, inc=1, device_id={"gx": (gx + k) % GX}, device_id_type=MESH)
        return carry

    lax.fori_loop(1, GX, greet, 0)
    for k in range(1, GY):
        pl.semaphore_signal(barrier, inc=1, device_id={"gy": (gy + k) % GY}, device_id_type=MESH)

    chunks = keys_ref.shape[0]
    hi_n, lo_n = ks_ref.shape
    ks = ks_ref[...]
    key_id = iota((hi_n, lo_n), 0) * lo_n + iota((hi_n, lo_n), 1)
    p1 = (ks >> 11) * 2 + ((ks >> 8) & 1)
    p1 = jnp.where(key_id == hk_ref[:, 0:1], 128, p1)
    p1 = jnp.where(key_id == hk_ref[:, 1:2], 129, p1)
    tab[0:lo_n, :] = p1.astype(F32).T.astype(BF16)
    tab[lo_n : 2 * lo_n, :] = (ks & 255).astype(F32).T.astype(BF16)
    pt[...] = jnp.zeros_like(pt)

    def look(c, carry):
        key = keys_ref[pl.ds(c, 1), :]
        hi, lo = key >> 8, key & 255
        t = dot(tab[...], onehot(hi_n, LANES, 0, hi))
        mine = iota((lo_n, LANES), 0) == lo
        a = jnp.sum(jnp.where(mine, t[:lo_n], 0.0), axis=0, keepdims=True).astype(I32)
        b = jnp.sum(jnp.where(mine, t[lo_n:], 0.0), axis=0, keepdims=True).astype(I32)
        heavy = a >= 128
        shi = jnp.where(heavy, -1, (a >> 1) * 8 + ((key >> 9) & 3) * 2 + (a & 1))
        shi_s[pl.ds(c, 1), :] = shi
        slo_s[pl.ds(c, 1), :] = b
        seg_s[pl.ds(c, 1), :] = jnp.where(
            heavy, GX * CAPK + (key >> 9) * 2 + (a - 128), (a >> 1) * CAPK
        )
        pt[...] += dot_t(onehot(lo_n, LANES, 0, b), onehot(hi_n, LANES, 0, shi))
        return carry

    lax.fori_loop(0, chunks, look, 0, unroll=2)

    here = jnp.where(pt[...] > 0.5, 1.0, 0.0).astype(BF16)
    lower = jnp.where(iota((lo_n, lo_n), 1) < iota((lo_n, lo_n), 0), 1.0, 0.0).astype(BF16)
    r0, r1 = iota((hi_n, hi_n), 0), iota((hi_n, hi_n), 1)
    before = jnp.where((r0 < r1) & ((r0 >> 3) == (r1 >> 3)), 1.0, 0.0).astype(BF16)
    column = dot(jnp.ones((lo_n, lo_n), BF16), here).astype(BF16)
    rk[...] = (dot(lower, here) + dot(column, before)).astype(BF16)

    def rank(c, carry):
        shi = shi_s[pl.ds(c, 1), :]
        slo = slo_s[pl.ds(c, 1), :]
        t = dot(rk[...], onehot(hi_n, LANES, 0, shi))
        mine = iota((lo_n, LANES), 0) == slo
        r = jnp.sum(jnp.where(mine, t, 0.0), axis=0, keepdims=True).astype(I32)
        seg_s[pl.ds(c, 1), :] = seg_s[pl.ds(c, 1), :] + jnp.where(shi < 0, 0, r)
        line = iota((W, LANES), 0)
        ext = jnp.where(line == 0, 1, jnp.where(line == 1, slo, jnp.where(line == 2, shi & 7, 0)))
        at = pl.ds(pl.multiple_of(c * LANES, LANES), LANES)
        xe[at, 0:W] = x_ref[at, :]
        xe[at, W : 2 * W] = ext.astype(F32).T.astype(BF16)
        return carry

    lax.fori_loop(0, chunks, rank, 0, unroll=2)

    half = chunks // 2

    def sums(bases, c):
        total = None
        for i in range(half):
            at = pl.ds(pl.multiple_of((c * half + i) * LANES, LANES), LANES)
            seg = seg_s[pl.ds(c * half + i, 1), :]
            oh = jnp.concatenate([onehot(W, LANES, b, seg) for b in bases], axis=0)
            part = dot(oh, xe[at, :])
            total = part if total is None else total + part
        return total

    lane = iota((512, W), 1)
    first = [GX * CAPK + i * W for i in range(4)]
    acc[...] = sums(first, 0)
    acc[...] += sums(first, 1)
    q, e = encode(acc[:, 0:W])
    hq[...] = q
    hx[...] = jnp.where(lane == 64, acc[:, W : W + 1], jnp.where(lane == 65, e, 0.0)).astype(I32)
    pl.semaphore_wait(barrier, GX + GY - 2)

    def to_owner(o):
        return pltpu.make_async_remote_copy(
            src_ref=msg.at[o], dst_ref=arr.at[gx], send_sem=ssem.at[o], recv_sem=rsem.at[gx],
            device_id={"gx": o}, device_id_type=MESH,
        )

    def send(m):
        def one(i, carry):
            o = pair_at(gx, i // 2, offset(m)) + i % 2

            @pl.when(o != gx)
            def _():
                to_owner(o).start()

            return carry

        lax.fori_loop(0, 8, one, 0)

    def owners(m, carry):
        pairs = [pair_at(gx, dx, offset(m)) for dx in range(4)]
        bases = [p * CAPK for p in pairs]
        acc[...] = sums(bases, 0)

        @pl.when(m > 0)
        def _():
            send(m - 1)

        acc[...] += sums(bases, 1)
        q, e = encode(acc[:, 0:W])
        t = jnp.where(lane == 3, e, acc[:, W : 2 * W]).T[0:8]
        cnt = t[0:1]
        slot = jnp.where(
            cnt > 0.5, jnp.floor((t[1:2] + 256.0 * t[2:3]) / jnp.maximum(cnt, 1.0) + 0.5), -1.0
        )
        line = iota((8, 512), 0)
        meta = jnp.where(line == 0, slot, jnp.where(line == 1, cnt, t[3:4])).astype(I32)
        for i in range(8):
            o = pairs[i // 2] + i % 2
            part = meta[:, (i // 2) * W : (i // 2 + 1) * W]
            if i % 2:
                part = pltpu.roll(part, 64, 1)
            at = pl.ds(pl.multiple_of(o * 8, 8), 8)
            part = jnp.where(iota((8, W), 1) < 64, part, hx[at, :])
            values = q[i * 64 : (i + 1) * 64].astype(I16)
            tail = jnp.concatenate([hq[at, :], part], axis=0).astype(I16)
            msg[pl.ds(o, 1), 0:64, :] = values[None]
            msg[pl.ds(o, 1), 64:80, :] = tail[None]

            @pl.when(o == gx)
            def _():
                arr[pl.ds(o, 1), 0:64, :] = values[None]
                arr[pl.ds(o, 1), 64:80, :] = tail[None]

        return carry

    lax.fori_loop(0, 8, owners, 0)

    for q in range(GY):
        at = slice(q * KD, (q + 1) * KD)
        scol[at, :] = slots_of(blocks_ref[:, at], gx) + q * KD
    send(7)

    dense[...] = jnp.zeros_like(dense)
    tal[...] = jnp.zeros_like(tal)
    hsum[...] = jnp.zeros_like(hsum)
    hcount[...] = jnp.zeros_like(hcount)
    lane8 = iota((8, W), 1)

    def arrive(m, carry):
        for dx in range(4):
            pair = pair_at(gx, -dx, -offset(m))
            metas = []
            for i in range(2):
                s = pair + i

                @pl.when(s != gx)
                def _():
                    pltpu.make_async_remote_copy(
                        src_ref=msg.at[s], dst_ref=arr.at[s], send_sem=ssem.at[s],
                        recv_sem=rsem.at[s], device_id={"gx": s}, device_id_type=MESH,
                    ).wait_recv()

                q = arr[pl.ds(s, 1), 0:64, :][0].astype(I32)
                high = q >> 8
                at = slice((dx * 2 + i) * 64, (dx * 2 + i + 1) * 64)
                v_s[at, 0:W] = high.astype(F32).astype(BF16)
                v_s[at, W : 2 * W] = (q - high * 256).astype(F32).astype(BF16)
                tail = arr[pl.ds(s, 1), 64:80, :][0].astype(I32)
                meta = tail[8:16]
                hsum[...] += tail[0:8].astype(F32) * power(meta[:, 65:66].astype(F32))
                hcount[...] += meta[:, 64:65].astype(F32) + jnp.zeros((8, W), F32)
                metas.append(meta)
            meta_s[:, dx * W : (dx + 1) * W] = jnp.where(
                lane8 < 64, metas[0], pltpu.roll(metas[1], 64, 1)
            )
        meta = meta_s[...]
        scale = power(meta[2:3].astype(F32))
        count = meta[1:2].astype(F32)

        def quarter(q, carry):
            at = pl.ds(pl.multiple_of(q * KD, KD), KD)
            mine = scol[at, :] == meta[0:1]
            dense[at, :] += dot(jnp.where(mine, scale, 0.0).astype(BF16), v_s[...])
            hits = jnp.where(mine, count, 0.0)
            tal[at, :] += (hits[:, 0:W] + hits[:, W : 2 * W]) + (
                hits[:, 2 * W : 3 * W] + hits[:, 3 * W : 4 * W]
            )
            return carry

        lax.fori_loop(0, GY, quarter, 0)
        return carry

    lax.fori_loop(0, 8, arrive, 0)

    line8 = iota((8, W), 0)
    for q in range(GY):
        rows = jnp.where(line8 == 0, hsum[2 * q : 2 * q + 1], 0.0)
        rows = jnp.where(line8 == 1, hsum[2 * q + 1 : 2 * q + 2], rows)
        rows = jnp.where(line8 == 2, hcount[2 * q : 2 * q + 1], rows)
        rows = jnp.where(line8 == 3, hcount[2 * q + 1 : 2 * q + 2], rows)
        quarters[q, KD + 8 : KD + 16, :] = rows

    def to_quarter(p):
        return pltpu.make_async_remote_copy(
            src_ref=quarters.at[p], dst_ref=parts.at[gy], send_sem=ysend.at[p],
            recv_sem=yrecv.at[gy], device_id={"gy": p}, device_id_type=MESH,
        )

    def leave(k, carry):
        p = (gy + k) % GY
        at = pl.ds(pl.multiple_of(p * KD, KD), KD)
        quarters[pl.ds(p, 1), 0:KD, :] = (dense[at, 0:W] * 256.0 + dense[at, W : 2 * W])[None]
        t = jnp.sum(tal[at, :].T, axis=0, keepdims=True)
        rows = jnp.zeros((8, W), F32)
        for i in range(4):
            rows = jnp.where(line8 == i, t[:, i * W : (i + 1) * W], rows)
        quarters[pl.ds(p, 1), KD : KD + 8, :] = rows[None]

        @pl.when(k > 1)
        def _():
            to_quarter((gy + k - 1) % GY).start()

        return carry

    lax.fori_loop(1, GY + 1, leave, 0)
    pos = slots_of(blocks_ref[:, pl.ds(pl.multiple_of(gy * KD, KD), KD)], gx)
    total = quarters[pl.ds(gy, 1), :, :][0]
    for k in range(1, GY):
        s = (gy + GY - k) % GY
        pltpu.make_async_remote_copy(
            src_ref=quarters.at[s], dst_ref=parts.at[s], send_sem=ysend.at[s],
            recv_sem=yrecv.at[s], device_id={"gy": s}, device_id_type=MESH,
        ).wait_recv()
        total = total + parts[pl.ds(s, 1), :, :][0]

    counts = total[KD : KD + 8]
    square = jnp.concatenate([counts, jnp.zeros((W - 8, W), F32)], axis=0).T
    col = jnp.concatenate([square[:, i : i + 1] for i in range(4)], axis=0)
    scaled[...] = (total[0:KD] * lax.rsqrt(1.0 + col)).reshape(GX, 8, W)

    def to_range(p):
        return pltpu.make_async_remote_copy(
            src_ref=scaled.at[p], dst_ref=moved_ref.at[gx], send_sem=fsend.at[p],
            recv_sem=frecv.at[gx], device_id={"gx": p}, device_id_type=MESH,
        )

    slots_ref[...] = jnp.sum(jnp.where(pos == iota((KD, KD), 1), col, 0.0), axis=0, keepdims=True)
    tail = total[KD + 8 : KD + 16]
    heavy_ref[...] = tail * lax.rsqrt(1.0 + pltpu.roll(tail, 6, 0))

    def range_out(k, carry):
        p = pair_at(gx, (k // 2) % 4, offset(k // 8)) + k % 2

        @pl.when(p != gx)
        def _():
            to_range(p).start()

        return carry

    lax.fori_loop(0, GX, range_out, 0)
    moved_ref[pl.ds(gx, 1), :, :] = scaled[pl.ds(gx, 1), :, :]

    def finish(k, carry):
        s = (gx + k) % GX
        to_owner(s).wait_send()
        to_range(s).wait_send()
        pltpu.make_async_remote_copy(
            src_ref=scaled.at[s], dst_ref=moved_ref.at[s], send_sem=fsend.at[s],
            recv_sem=frecv.at[s], device_id={"gx": s}, device_id_type=MESH,
        ).wait_recv()
        return carry

    lax.fori_loop(1, GX, finish, 0)
    for k in range(1, GY):
        to_quarter((gy + k) % GY).wait_send()


def join(keys, x, ks, hk, blocks):
    rows = x.shape[0]
    chunks = rows // LANES
    dma = pltpu.SemaphoreType.DMA
    return pl.pallas_call(
        join_kernel,
        out_shape=(
            jax.ShapeDtypeStruct((GX, 8, W), F32),
            jax.ShapeDtypeStruct((1, KD), F32),
            jax.ShapeDtypeStruct((8, W), F32),
        ),
        in_specs=[VMEM] * 5,
        out_specs=(VMEM,) * 3,
        scratch_shapes=[
            pltpu.VMEM((512, 512), BF16),
            pltpu.VMEM((chunks, LANES), I32),
            pltpu.VMEM((chunks, LANES), I32),
            pltpu.VMEM((chunks, LANES), I32),
            pltpu.VMEM((rows, 2 * W), BF16),
            pltpu.VMEM((256, 512), F32),
            pltpu.VMEM((256, 512), BF16),
            pltpu.VMEM((512, 2 * W), F32),
            pltpu.VMEM((512, W), I32),
            pltpu.VMEM((512, W), I32),
            pltpu.VMEM((GX, MSG, W), I16),
            pltpu.VMEM((GX, MSG, W), I16),
            pltpu.VMEM((512, 2 * W), BF16),
            pltpu.VMEM((8, 512), I32),
            pltpu.VMEM((OWN, 1), I32),
            pltpu.VMEM((OWN, 2 * W), F32),
            pltpu.VMEM((OWN, W), F32),
            pltpu.VMEM((8, W), F32),
            pltpu.VMEM((8, W), F32),
            pltpu.VMEM((GY, KD + 16, W), F32),
            pltpu.VMEM((GY, KD + 16, W), F32),
            pltpu.VMEM((GX, 8, W), F32),
            dma((GX,)), dma((GX,)), dma((GY,)), dma((GY,)), dma((GX,)), dma((GX,)),
        ],
        compiler_params=pltpu.CompilerParams(
            collective_id=0, has_side_effects=True, vmem_limit_bytes=56 * 2**20
        ),
        name="join_rows",
    )(keys, x, ks, hk, blocks)


def result_kernel(got_ref, orders_ref, row_ref, col_ref, hloc_ref, heavy_ref, out_ref, report_ref):
    own_row = row_ref[...] >> 11
    own_col = col_ref[...] >> 11
    j0, j1 = iota((KD, KD), 0), iota((KD, KD), 1)
    w = jnp.sum(jnp.where((own_row == own_col) & (j1 < j0), 1.0, 0.0), axis=1, keepdims=True)
    place = own_col * 8 + w.astype(I32)
    oh = jnp.where(place == j1, 1.0, 0.0).astype(BF16)
    got = got_ref[...]
    high = got.astype(BF16)
    low = (got - high.astype(F32)).astype(BF16)
    total = dot(oh, high) + dot(oh, low)
    orders = orders_ref[...].astype(F32)
    line = iota((KD, W), 0)
    reports = []
    for h in range(2):
        here = line == hloc_ref[h]
        total = jnp.where(here, heavy_ref[h : h + 1, :], total)
        mine = jnp.sum(jnp.where(here, orders, 0.0), axis=0, keepdims=True)
        reports.append(mine * heavy_ref[h : h + 1, :])
    out_ref[...] = (orders * total).astype(BF16)
    report_ref[...] = jnp.concatenate(reports, axis=0).astype(BF16)


def outputs(got, orders, row, col, hloc, heavy):
    return pl.pallas_call(
        result_kernel,
        out_shape=(jax.ShapeDtypeStruct((KD, W), BF16), jax.ShapeDtypeStruct((2, W), BF16)),
        in_specs=[VMEM, VMEM, VMEM, VMEM, pl.BlockSpec(memory_space=pltpu.SMEM), VMEM],
        out_specs=(VMEM, VMEM),
        compiler_params=pltpu.CompilerParams(vmem_limit_bytes=32 * 2**20),
        name="range_outputs",
    )(got, orders, row, col, hloc, heavy)


def body(measures, row_keys, orders, heavy_keys, key_slot):
    device = lax.axis_index("gx") * GY + lax.axis_index("gy")
    rows = measures.shape[0]
    keys = row_keys.reshape(rows // LANES, LANES)
    pairs = jnp.repeat(heavy_keys.reshape(-1, 2), 2, axis=0)
    blocks = key_slot.reshape(GX, GY * KD)
    moved, slot_rows, heavy = join(
        keys, measures, key_slot.reshape(KEYS // 256, 256), pairs, blocks
    )
    own_slots = lax.dynamic_slice_in_dim(key_slot, device * KD, KD)
    heavy_local = lax.dynamic_slice_in_dim(heavy_keys, device * 2, 2) - device * KD
    result, report = outputs(
        moved.reshape(KD, W), orders, own_slots.reshape(1, KD), own_slots.reshape(KD, 1),
        heavy_local, heavy,
    )
    return (result, report, slot_rows.reshape(KD))


def solution(mesh):
    return jax.shard_map(
        body,
        mesh=mesh,
        in_specs=(P(("gx", "gy"), None), P(("gx", "gy")), P(("gx", "gy"), None), P(), P()),
        out_specs=(P(("gx", "gy"), None), P(("gx", "gy"), None), P(("gx", "gy"))),
        check_vma=False,
    )
```

time: 157 us -> 130 us (0.83)
  Pallas kernels: 152 us -> 117 us
  local copies, waits for them, and re-layouts: 3.22 us -> 10.7 us
    pallas_call x6 -> x1, Pallas kernels: 149 us -> 115 us  [join(): pl.pallas_call(join_kernel, out_shape=(jax.ShapeDtypeStruct((GX, 8, W), F...]
    unnamed x4 -> x7, local copies, waits for them, and re-layouts: 0.01 us -> 2.9 us
    reshape x1, local copies, waits for them, and re-layouts: 0.08 us -> 1.92 us  [body(): blocks = key_slot.reshape(GX, GY * KD)]
where the time goes in v2:
time: 130 us
  Pallas kernels  117 us (90%)
  local copies, waits for them, and re-layouts  10.7 us (8%)
    pallas_call x1, Pallas kernels, join(): pl.pallas_call(join_kernel, out_shape=(jax.ShapeDtypeStruct((GX, 8, W), F...  115 us
    unnamed x7, local copies, waits for them, and re-layouts  2.9 us

profile of v2, /device:TPU:1, one launch (start us, length us, event | category | flops | bytes accessed | tf_op | source)
XLA Modules:
  0.0 129.5 jit_solution(12025003067782588593)
XLA Ops:
  0.6 1.4 %reshape.33.keys_ref = s32[8,1024]{1,0:T(8,128)} reshape(s32[8192]{0:T(1024)} %param.6) | data formatting | bytes 65536 | tf_op jit(solution)/shard_map/reshape | solution.py:450
  2.0 2.0 %reshape.34.ks_ref = s32[512,256]{1,0:T(8,128)} reshape(s32[131072]{0:T(1024)} %param.9) | data formatting | bytes 1048576 | tf_op jit(solution)/shard_map/reshape | solution.py:454
  4.0 0.8 reshape.35
  4.8 0.8 broadcast_in_dim.3
  5.6 1.9 %reshape.37.blocks_ref = s32[64,2048]{1,0:T(8,128)} reshape(s32[131072]{0:T(1024)} %param.9) | data formatting | bytes 1048576 | tf_op jit(solution)/shard_map/reshape | solution.py:452
  7.5 0.0 copy-start.1
  7.5 115.2 %join_rows.1 = (f32[64,8,128]{2,1,0:T(8,128)}, f32[1,512]{1,0:T(1,128)}, f32[8,128]{1,0:T(8,128)}) custom-call(s32[8,1024]{1,0:T(8,128)} %reshape.33.keys_ref, bf16[8192,128]{1,0:T(8,128)(2,1)} %x_ref.1, s32[512,256]{1,0:T(8,128)} %reshape.34.ks_ref, s32[512,2]{1,0:T(8,128)} %bitcast.8, s32[64,2048]{1,0:T(8,128)} %reshape.37.blocks_ref), custom_call_target="tpu_custom_call" | custom-call | tf_op jit(solution)/shard_map/join_rows/pallas_call | solution.py:372
  122.8 0.8 dynamic_slice.6
  123.5 0.1 copy.8.col_ref
  123.7 0.8 dynamic-slice_subtract_fusion.hloc_ref
  124.5 0.0 copy-done.1
  124.5 0.0 copy-start
  124.5 0.9 copy-done
  125.4 0.0 copy-start.2
  125.4 0.7 copy-done.2
  126.1 2.2 %range_outputs.1 = (bf16[512,128]{1,0:T(8,128)(2,1)}, bf16[2,128]{1,0:T(2,128)(2,1)}) custom-call(f32[512,128]{1,0:T(8,128)S(1)} %bitcast.5, bf16[512,128]{1,0:T(8,128)(2,1)S(1)} %copy-done.1, s32[1,512]{1,0:T(1,128)S(1)} %bitcast.7, s32[512,1]{1,0:T(8,128)S(1)} %copy.8.col_ref, s32[2]{0:T(128)S(1)} %dynamic-slice_subtract_fusion.hloc_ref, ...), custom_call_target="tpu_custom_call" | custom-call | tf_op jit(solution)/shard_map/range_outputs/pallas_call | solution.py:437
  128.3 1.3 copy.10
Async XLA Ops:
  7.5 116.9 %copy-start.1 = (bf16[512,128]{1,0:T(8,128)(2,1)S(1)}, bf16[512,128]{1,0:T(8,128)(2,1)}, u32[]{:S(2)}) copy-start(bf16[512,128]{1,0:T(8,128)(2,1)} %orders_ref.1) | copy-start | bytes 393220
  124.5 1.0 copy-start
  125.4 0.7 copy-start.2

commit v3 on v2

--- a/solution.py
+++ b/solution.py
@@ -48,6 +48,11 @@
     e = jnp.maximum(e, -100.0)
     q = jnp.floor(v * power(-e) + 0.5).astype(I32)
     return q, e
+
+
+def quarter_of(ks_ref, q):
+    rows = [ks_ref[pl.ds(q * 4 + i, GX, stride=16), :] for i in range(4)]
+    return jnp.concatenate(rows, axis=1)
 
 
 def slots_of(ks, me):
@@ -78,13 +83,15 @@
     return (((x + 4 + dx) % 4) * 8 + (z + 8 + dz) % 8) * 2
 
 
-def join_kernel(keys_ref, x_ref, ks_ref, hk_ref, blocks_ref,
-                moved_ref, slots_ref, heavy_ref,
+def join_kernel(keys_ref, x_ref, ks_ref, hk_ref, heavy_ref, orders_ref,
+                out_ref, report_ref, slots_ref,
                 tab, shi_s, slo_s, seg_s, xe, pt, rk, acc, hq, hx, msg, arr,
-                v_s, meta_s, scol, dense, tal, hsum, hcount, quarters, parts, scaled,
-                ssem, rsem, ysend, yrecv, fsend, frecv):
+                v_s, meta_s, scol, dense, tal, hsum, hcount, quarters, parts, hquart, hparts,
+                scaled, moved, place_s, ssem, rsem, ysend, yrecv, hsend, hrecv, fsend, frecv, xsem):
     gx, gy = lax.axis_index("gx"), lax.axis_index("gy")
     barrier = pltpu.get_barrier_semaphore()
+    rows_in = pltpu.make_async_copy(x_ref, xe.at[:, 0:W], xsem)
+    rows_in.start()
 
     def greet(k, carry):
         pl.semaphore_signal(barrier, inc=1, device_id={"gx": (gx + k) % GX}, device_id_type=MESH)
@@ -94,30 +101,49 @@
     for k in range(1, GY):
         pl.semaphore_signal(barrier, inc=1, device_id={"gy": (gy + k) % GY}, device_id_type=MESH)
 
-    chunks = keys_ref.shape[0]
-    hi_n, lo_n = ks_ref.shape
-    ks = ks_ref[...]
-    key_id = iota((hi_n, lo_n), 0) * lo_n + iota((hi_n, lo_n), 1)
-    p1 = (ks >> 11) * 2 + ((ks >> 8) & 1)
-    p1 = jnp.where(key_id == hk_ref[:, 0:1], 128, p1)
-    p1 = jnp.where(key_id == hk_ref[:, 1:2], 129, p1)
-    tab[0:lo_n, :] = p1.astype(F32).T.astype(BF16)
-    tab[lo_n : 2 * lo_n, :] = (ks & 255).astype(F32).T.astype(BF16)
+    chunks = xe.shape[0] // LANES
+    hi_n, lo_n = 512, 256
+    for i in range(2):
+        ks = ks_ref[pl.ds(i, hi_n, stride=2), :]
+        p1 = (ks >> 11) * 2 + ((ks >> 8) & 1)
+        tab[i * W : (i + 1) * W, :] = p1.astype(F32).T.astype(BF16)
+        tab[lo_n + i * W : lo_n + (i + 1) * W, :] = (ks & 255).astype(F32).T.astype(BF16)
+    hk = jnp.concatenate([hk_ref[i : i + 1, :] for i in range(4)], axis=1)
+    line = iota((16, hi_n), 0)
+    digits = jnp.where(line == 0, hk & 255, jnp.where(line == 1, (hk >> 8) & 1, 0))
+    digits = digits.astype(F32).astype(BF16)
+    block = 2 * (iota((hi_n, hi_n), 1) >> 1)
+    odd = (iota((1, hi_n), 1) & 1).astype(F32)
+    marks = jnp.full((16, hi_n), -1.0, F32)
+    for i in range(2):
+        pick = jnp.where(iota((hi_n, hi_n), 0) == block + i, 1.0, 0.0).astype(BF16)
+        found = dot(digits, pick)
+        marks = jnp.where(line == i, jnp.where(found[1:2] == odd, found[0:1], -1.0), marks)
+    tab[2 * lo_n : 2 * lo_n + 16, :] = marks.astype(BF16)
+    z0, x0 = (gx // 2) % 8, gx // 16
     pt[...] = jnp.zeros_like(pt)
 
     def look(c, carry):
-        key = keys_ref[pl.ds(c, 1), :]
+        block = keys_ref[pl.ds(pl.multiple_of(c * 8, 8), 8), :]
+        key = jnp.concatenate([block[i : i + 1] for i in range(8)], axis=1)
         hi, lo = key >> 8, key & 255
         t = dot(tab[...], onehot(hi_n, LANES, 0, hi))
         mine = iota((lo_n, LANES), 0) == lo
         a = jnp.sum(jnp.where(mine, t[:lo_n], 0.0), axis=0, keepdims=True).astype(I32)
-        b = jnp.sum(jnp.where(mine, t[lo_n:], 0.0), axis=0, keepdims=True).astype(I32)
-        heavy = a >= 128
-        shi = jnp.where(heavy, -1, (a >> 1) * 8 + ((key >> 9) & 3) * 2 + (a & 1))
+        b = jnp.sum(jnp.where(mine, t[lo_n : 2 * lo_n], 0.0), axis=0, keepdims=True).astype(I32)
+        low = lo.astype(F32)
+        second = t[2 * lo_n + 1 : 2 * lo_n + 2] == low
+        heavy = (t[2 * lo_n : 2 * lo_n + 1] == low) | second
+        owner = a >> 1
+        dx = ((owner >> 4) + 4 - x0) & 3
+        dz = (((owner >> 1) & 7) + 8 - z0) & 7
+        zi = jnp.where(dz == 0, 0, jnp.where(dz <= 4, 2 * dz - 1, 16 - 2 * dz))
+        place = (7 - zi) * 8 + dx * 2 + (owner & 1)
+        shi = jnp.where(heavy, -1, owner * 8 + ((key >> 9) & 3) * 2 + (a & 1))
         shi_s[pl.ds(c, 1), :] = shi
         slo_s[pl.ds(c, 1), :] = b
         seg_s[pl.ds(c, 1), :] = jnp.where(
-            heavy, GX * CAPK + (key >> 9) * 2 + (a - 128), (a >> 1) * CAPK
+            heavy, GX * CAPK + (key >> 9) * 2 + jnp.where(second, 1, 0), place * CAPK
         )
         pt[...] += dot_t(onehot(lo_n, LANES, 0, b), onehot(hi_n, LANES, 0, shi))
         return carry
@@ -141,7 +167,6 @@
         line = iota((W, LANES), 0)
         ext = jnp.where(line == 0, 1, jnp.where(line == 1, slo, jnp.where(line == 2, shi & 7, 0)))
         at = pl.ds(pl.multiple_of(c * LANES, LANES), LANES)
-        xe[at, 0:W] = x_ref[at, :]
         xe[at, W : 2 * W] = ext.astype(F32).T.astype(BF16)
         return carry
 
@@ -149,20 +174,17 @@
 
     half = chunks // 2
 
-    def sums(bases, c):
+    def sums(base, c):
         total = None
         for i in range(half):
             at = pl.ds(pl.multiple_of((c * half + i) * LANES, LANES), LANES)
-            seg = seg_s[pl.ds(c * half + i, 1), :]
-            oh = jnp.concatenate([onehot(W, LANES, b, seg) for b in bases], axis=0)
-            part = dot(oh, xe[at, :])
+            part = dot(onehot(512, LANES, base, seg_s[pl.ds(c * half + i, 1), :]), xe[at, :])
             total = part if total is None else total + part
         return total
 
+    rows_in.wait()
     lane = iota((512, W), 1)
-    first = [GX * CAPK + i * W for i in range(4)]
-    acc[...] = sums(first, 0)
-    acc[...] += sums(first, 1)
+    acc[...] = sums(GX * CAPK, 0) + sums(GX * CAPK, 1)
     q, e = encode(acc[:, 0:W])
     hq[...] = q
     hx[...] = jnp.where(lane == 64, acc[:, W : W + 1], jnp.where(lane == 65, e, 0.0)).astype(I32)
@@ -188,14 +210,16 @@
 
     def owners(m, carry):
         pairs = [pair_at(gx, dx, offset(m)) for dx in range(4)]
-        bases = [p * CAPK for p in pairs]
-        acc[...] = sums(bases, 0)
-
-        @pl.when(m > 0)
-        def _():
-            send(m - 1)
-
-        acc[...] += sums(bases, 1)
+
+        def step(c, carry):
+            @pl.when((c > 0) & (m > 0))
+            def _():
+                send(m - 1)
+
+            acc[...] = jnp.where(c > 0, acc[...], 0.0) + sums(m * 512, c)
+            return carry
+
+        lax.fori_loop(0, 2, step, 0)
         q, e = encode(acc[:, 0:W])
         t = jnp.where(lane == 3, e, acc[:, W : 2 * W]).T[0:8]
         cnt = t[0:1]
@@ -227,7 +251,7 @@
 
     for q in range(GY):
         at = slice(q * KD, (q + 1) * KD)
-        scol[at, :] = slots_of(blocks_ref[:, at], gx) + q * KD
+        scol[at, :] = slots_of(quarter_of(ks_ref, q), gx) + q * KD
     send(7)
 
     dense[...] = jnp.zeros_like(dense)
@@ -267,17 +291,14 @@
         scale = power(meta[2:3].astype(F32))
         count = meta[1:2].astype(F32)
 
-        def quarter(q, carry):
-            at = pl.ds(pl.multiple_of(q * KD, KD), KD)
+        for q in range(GY):
+            at = slice(q * KD, (q + 1) * KD)
             mine = scol[at, :] == meta[0:1]
             dense[at, :] += dot(jnp.where(mine, scale, 0.0).astype(BF16), v_s[...])
             hits = jnp.where(mine, count, 0.0)
             tal[at, :] += (hits[:, 0:W] + hits[:, W : 2 * W]) + (
                 hits[:, 2 * W : 3 * W] + hits[:, 3 * W : 4 * W]
             )
-            return carry
-
-        lax.fori_loop(0, GY, quarter, 0)
         return carry
 
     lax.fori_loop(0, 8, arrive, 0)
@@ -288,7 +309,7 @@
         rows = jnp.where(line8 == 1, hsum[2 * q + 1 : 2 * q + 2], rows)
         rows = jnp.where(line8 == 2, hcount[2 * q : 2 * q + 1], rows)
         rows = jnp.where(line8 == 3, hcount[2 * q + 1 : 2 * q + 2], rows)
-        quarters[q, KD + 8 : KD + 16, :] = rows
+        hquart[q, :, :] = rows
 
     def to_quarter(p):
         return pltpu.make_async_remote_copy(
@@ -296,47 +317,84 @@
             recv_sem=yrecv.at[gy], device_id={"gy": p}, device_id_type=MESH,
         )
 
+    def heavy_to(p):
+        return pltpu.make_async_remote_copy(
+            src_ref=hquart.at[p], dst_ref=hparts.at[gy], send_sem=hsend.at[p],
+            recv_sem=hrecv.at[gy], device_id={"gy": p}, device_id_type=MESH,
+        )
+
     def leave(k, carry):
         p = (gy + k) % GY
         at = pl.ds(pl.multiple_of(p * KD, KD), KD)
-        quarters[pl.ds(p, 1), 0:KD, :] = (dense[at, 0:W] * 256.0 + dense[at, W : 2 * W])[None]
+        q, e = encode(dense[at, 0:W] * 256.0 + dense[at, W : 2 * W])
+        q = q.astype(I16)
         t = jnp.sum(tal[at, :].T, axis=0, keepdims=True)
-        rows = jnp.zeros((8, W), F32)
+        e = jnp.where(lane == 0, e, 0.0).T[0:1]
+        line = iota((16, W), 0)
+        rows = jnp.zeros((16, W), F32)
         for i in range(4):
-            rows = jnp.where(line8 == i, t[:, i * W : (i + 1) * W], rows)
-        quarters[pl.ds(p, 1), KD : KD + 8, :] = rows[None]
+            rows = jnp.where(line == i, t[:, i * W : (i + 1) * W], rows)
+            rows = jnp.where(line == 4 + i, e[:, i * W : (i + 1) * W], rows)
+        rows = rows.astype(I32).astype(I16)
+        quarters[pl.ds(p, 1), 0:KD, :] = q[None]
+        quarters[pl.ds(p, 1), KD : KD + 16, :] = rows[None]
 
         @pl.when(k > 1)
         def _():
             to_quarter((gy + k - 1) % GY).start()
 
+        @pl.when(k == GY)
+        def _():
+            parts[pl.ds(gy, 1), 0:KD, :] = q[None]
+            parts[pl.ds(gy, 1), KD : KD + 16, :] = rows[None]
+
         return carry
 
     lax.fori_loop(1, GY + 1, leave, 0)
-    pos = slots_of(blocks_ref[:, pl.ds(pl.multiple_of(gy * KD, KD), KD)], gx)
-    total = quarters[pl.ds(gy, 1), :, :][0]
     for k in range(1, GY):
+        heavy_to((gy + k) % GY).start()
+    pos = slots_of(quarter_of(ks_ref, gy), gx)
+
+    device = gx * GY + gy
+    owners_here = [ks_ref[pl.ds(device * 4 + i, 1), :] >> 11 for i in range(4)]
+    row = jnp.concatenate(owners_here, axis=1)
+    square = jnp.zeros((W, W), I32)
+    for i in range(4):
+        square = jnp.where(iota((W, W), 0) == i, owners_here[i], square)
+    square = square.astype(F32).T.astype(I32)
+    col = jnp.concatenate([square[:, i : i + 1] for i in range(4)], axis=0)
+    j0, j1 = iota((KD, KD), 0), iota((KD, KD), 1)
+    w = jnp.sum(jnp.where((row == col) & (j1 < j0), 1.0, 0.0), axis=1, keepdims=True)
+    place_s[...] = jnp.where(col * 8 + w.astype(I32) == j1, 1.0, 0.0).astype(BF16)
+
+    total, tallies = jnp.zeros((KD, W), F32), jnp.zeros((W, W), F32)
+    tail = hquart[pl.ds(gy, 1), :, :][0]
+    for k in range(GY):
         s = (gy + GY - k) % GY
-        pltpu.make_async_remote_copy(
-            src_ref=quarters.at[s], dst_ref=parts.at[s], send_sem=ysend.at[s],
-            recv_sem=yrecv.at[s], device_id={"gy": s}, device_id_type=MESH,
-        ).wait_recv()
-        total = total + parts[pl.ds(s, 1), :, :][0]
-
-    counts = total[KD : KD + 8]
-    square = jnp.concatenate([counts, jnp.zeros((W - 8, W), F32)], axis=0).T
-    col = jnp.concatenate([square[:, i : i + 1] for i in range(4)], axis=0)
-    scaled[...] = (total[0:KD] * lax.rsqrt(1.0 + col)).reshape(GX, 8, W)
+        if k:
+            for sent, got, ss, rs in ((quarters, parts, ysend, yrecv), (hquart, hparts, hsend, hrecv)):
+                pltpu.make_async_remote_copy(
+                    src_ref=sent.at[s], dst_ref=got.at[s], send_sem=ss.at[s], recv_sem=rs.at[s],
+                    device_id={"gy": s}, device_id_type=MESH,
+                ).wait_recv()
+            tail = tail + hparts[pl.ds(s, 1), :, :][0]
+        rows = parts[pl.ds(s, 1), KD : KD + 16, :][0].astype(F32)
+        square = jnp.concatenate([rows, jnp.zeros((W - 16, W), F32)], axis=0).T
+        scale = jnp.concatenate([square[:, 4 + i : 5 + i] for i in range(4)], axis=0)
+        total = total + parts[pl.ds(s, 1), 0:KD, :][0].astype(F32) * power(scale)
+        tallies = tallies + square
+
+    col = jnp.concatenate([tallies[:, i : i + 1] for i in range(4)], axis=0)
+    scaled[...] = (total * lax.rsqrt(1.0 + col)).reshape(GX, 8, W)
 
     def to_range(p):
         return pltpu.make_async_remote_copy(
-            src_ref=scaled.at[p], dst_ref=moved_ref.at[gx], send_sem=fsend.at[p],
+            src_ref=scaled.at[p], dst_ref=moved.at[gx], send_sem=fsend.at[p],
             recv_sem=frecv.at[gx], device_id={"gx": p}, device_id_type=MESH,
         )
 
-    slots_ref[...] = jnp.sum(jnp.where(pos == iota((KD, KD), 1), col, 0.0), axis=0, keepdims=True)
-    tail = total[KD + 8 : KD + 16]
-    heavy_ref[...] = tail * lax.rsqrt(1.0 + pltpu.roll(tail, 6, 0))
+    slots = jnp.sum(jnp.where(pos == j1, col, 0.0), axis=0, keepdims=True)
+    slots_ref[...] = jnp.concatenate([slots[:, i * W : (i + 1) * W] for i in range(4)], axis=0)
 
     def range_out(k, carry):
         p = pair_at(gx, (k // 2) % 4, offset(k // 8)) + k % 2
@@ -348,14 +406,14 @@
         return carry
 
     lax.fori_loop(0, GX, range_out, 0)
-    moved_ref[pl.ds(gx, 1), :, :] = scaled[pl.ds(gx, 1), :, :]
+    moved[pl.ds(gx, 1), :, :] = scaled[pl.ds(gx, 1), :, :]
 
     def finish(k, carry):
         s = (gx + k) % GX
         to_owner(s).wait_send()
         to_range(s).wait_send()
         pltpu.make_async_remote_copy(
-            src_ref=scaled.at[s], dst_ref=moved_ref.at[s], send_sem=fsend.at[s],
+            src_ref=scaled.at[s], dst_ref=moved.at[s], send_sem=fsend.at[s],
             recv_sem=frecv.at[s], device_id={"gx": s}, device_id_type=MESH,
         ).wait_recv()
         return carry
@@ -363,23 +421,44 @@
     lax.fori_loop(1, GX, finish, 0)
     for k in range(1, GY):
         to_quarter((gy + k) % GY).wait_send()
-
-
-def join(keys, x, ks, hk, blocks):
+        heavy_to((gy + k) % GY).wait_send()
+
+    got = moved[...].reshape(KD, W)
+    high = got.astype(BF16)
+    low = (got - high.astype(F32)).astype(BF16)
+    both = dot(place_s[...], jnp.concatenate([high, low], axis=1))
+    total = both[:, 0:W] + both[:, W : 2 * W]
+    orders = orders_ref[...].astype(F32)
+    heavy = tail * lax.rsqrt(1.0 + pltpu.roll(tail, 6, 0))
+    line = iota((KD, W), 0)
+    reports = []
+    for h in range(2):
+        here = line == heavy_ref[2 * device + h] - device * KD
+        total = jnp.where(here, heavy[h : h + 1, :], total)
+        mine = jnp.sum(jnp.where(here, orders, 0.0), axis=0, keepdims=True)
+        reports.append(mine * heavy[h : h + 1, :])
+    out_ref[...] = (orders * total).astype(BF16)
+    report_ref[...] = jnp.concatenate(reports, axis=0).astype(BF16)
+
+
+def join(keys, x, ks, heavy_keys, orders):
     rows = x.shape[0]
     chunks = rows // LANES
     dma = pltpu.SemaphoreType.DMA
     return pl.pallas_call(
         join_kernel,
         out_shape=(
-            jax.ShapeDtypeStruct((GX, 8, W), F32),
-            jax.ShapeDtypeStruct((1, KD), F32),
-            jax.ShapeDtypeStruct((8, W), F32),
+            jax.ShapeDtypeStruct((KD, W), BF16),
+            jax.ShapeDtypeStruct((2, W), BF16),
+            jax.ShapeDtypeStruct((4, W), F32),
         ),
-        in_specs=[VMEM] * 5,
+        in_specs=[
+            VMEM, pl.BlockSpec(memory_space=pl.ANY), VMEM, VMEM,
+            pl.BlockSpec(memory_space=pltpu.SMEM), VMEM,
+        ],
         out_specs=(VMEM,) * 3,
         scratch_shapes=[
-            pltpu.VMEM((512, 512), BF16),
+            pltpu.VMEM((528, 512), BF16),
             pltpu.VMEM((chunks, LANES), I32),
             pltpu.VMEM((chunks, LANES), I32),
             pltpu.VMEM((chunks, LANES), I32),
@@ -398,67 +477,44 @@
             pltpu.VMEM((OWN, W), F32),
             pltpu.VMEM((8, W), F32),
             pltpu.VMEM((8, W), F32),
-            pltpu.VMEM((GY, KD + 16, W), F32),
-            pltpu.VMEM((GY, KD + 16, W), F32),
+            pltpu.VMEM((GY, KD + 16, W), I16),
+            pltpu.VMEM((GY, KD + 16, W), I16),
+            pltpu.VMEM((GY, 8, W), F32),
+            pltpu.VMEM((GY, 8, W), F32),
             pltpu.VMEM((GX, 8, W), F32),
-            dma((GX,)), dma((GX,)), dma((GY,)), dma((GY,)), dma((GX,)), dma((GX,)),
+            pltpu.VMEM((GX, 8, W), F32),
+            pltpu.VMEM((KD, KD), BF16),
+            dma((GX,)), dma((GX,)), dma((GY,)), dma((GY,)), dma((GY,)), dma((GY,)),
+            dma((GX,)), dma((GX,)), dma,
         ],
         compiler_params=pltpu.CompilerParams(
             collective_id=0, has_side_effects=True, vmem_limit_bytes=56 * 2**20
         ),
         name="join_rows",
-    )(keys, x, ks, hk, blocks)
-
-
-def result_kernel(got_ref, orders_ref, row_ref, col_ref, hloc_ref, heavy_ref, out_ref, report_ref):
-    own_row = row_ref[...] >> 11
-    own_col = col_ref[...] >> 11
-    j0, j1 = iota((KD, KD), 0), iota((KD, KD), 1)
-    w = jnp.sum(jnp.where((own_row == own_col) & (j1 < j0), 1.0, 0.0), axis=1, keepdims=True)
-    place = own_col * 8 + w.astype(I32)
-    oh = jnp.where(place == j1, 1.0, 0.0).astype(BF16)
-    got = got_ref[...]
-    high = got.astype(BF16)
-    low = (got - high.astype(F32)).astype(BF16)
-    total = dot(oh, high) + dot(oh, low)
-    orders = orders_ref[...].astype(F32)
-    line = iota((KD, W), 0)
-    reports = []
-    for h in range(2):
-        here = line == hloc_ref[h]
-        total = jnp.where(here, heavy_ref[h : h + 1, :], total)
-        mine = jnp.sum(jnp.where(here, orders, 0.0), axis=0, keepdims=True)
-        reports.append(mine * heavy_ref[h : h + 1, :])
-    out_ref[...] = (orders * total).astype(BF16)
-    report_ref[...] = jnp.concatenate(reports, axis=0).astype(BF16)
-
-
-def outputs(got, orders, row, col, hloc, heavy):
+    )(keys, x, ks, heavy_keys.reshape(-1, W), heavy_keys, orders)
+
+
+def hand_on_kernel(a_ref, b_ref, c_ref, out_a, out_b, out_c):
+    out_a[...] = a_ref[...]
+    out_b[...] = b_ref[...]
+    out_c[...] = c_ref[...]
+
+
+def hand_on(*arrays):
     return pl.pallas_call(
-        result_kernel,
-        out_shape=(jax.ShapeDtypeStruct((KD, W), BF16), jax.ShapeDtypeStruct((2, W), BF16)),
-        in_specs=[VMEM, VMEM, VMEM, VMEM, pl.BlockSpec(memory_space=pltpu.SMEM), VMEM],
-        out_specs=(VMEM, VMEM),
-        compiler_params=pltpu.CompilerParams(vmem_limit_bytes=32 * 2**20),
-        name="range_outputs",
-    )(got, orders, row, col, hloc, heavy)
+        hand_on_kernel,
+        out_shape=tuple(jax.ShapeDtypeStruct(a.shape, a.dtype) for a in arrays),
+        in_specs=[VMEM] * 3,
+        out_specs=(VMEM,) * 3,
+        name="hand_on",
+    )(*arrays)
 
 
 def body(measures, row_keys, orders, heavy_keys, key_slot):
-    device = lax.axis_index("gx") * GY + lax.axis_index("gy")
-    rows = measures.shape[0]
-    keys = row_keys.reshape(rows // LANES, LANES)
-    pairs = jnp.repeat(heavy_keys.reshape(-1, 2), 2, axis=0)
-    blocks = key_slot.reshape(GX, GY * KD)
-    moved, slot_rows, heavy = join(
-        keys, measures, key_slot.reshape(KEYS // 256, 256), pairs, blocks
+    result, report, slot_rows = join(
+        row_keys.reshape(-1, W), measures, key_slot.reshape(-1, W), heavy_keys, orders
     )
-    own_slots = lax.dynamic_slice_in_dim(key_slot, device * KD, KD)
-    heavy_local = lax.dynamic_slice_in_dim(heavy_keys, device * 2, 2) - device * KD
-    result, report = outputs(
-        moved.reshape(KD, W), orders, own_slots.reshape(1, KD), own_slots.reshape(KD, 1),
-        heavy_local, heavy,
-    )
+    result, report, slot_rows = hand_on(result, report, slot_rows)
     return (result, report, slot_rows.reshape(KD))
 
 

time: 130 us -> 93.1 us (0.72)
  Pallas kernels: 117 us -> 92.4 us
  local copies, waits for them, and re-layouts: 10.7 us -> 0 us
    pallas_call x2, Pallas kernels: 117 us -> 92.4 us  [the longest x1 90.8 us: join(): pl.pallas_call(join_kernel, out_shape=(jax.ShapeDtypeStruct((KD, W), BF16...]
    reshape x5 -> x0, local copies, waits for them, and re-layouts: 6.25 us -> none  [the longest x1 1.98 us: body(): key_slot.reshape(KEYS // 256, 256)]
    unnamed x7 -> x0, local copies, waits for them, and re-layouts: 2.9 us -> none
where the time goes in v3:
time: 93.1 us; the launch traced here: 93 us
  Pallas kernels  92.4 us (99%)
    pallas_call x1, Pallas kernels, join(): pl.pallas_call(join_kernel, out_shape=(jax.ShapeDtypeStruct((KD, W), BF16...  90.8 us

profile of v3, /device:TPU:1, one launch (start us, length us, event | category | flops | bytes accessed | tf_op | source)
XLA Modules:
  0.0 93.0 jit_solution(11561938291066221816)
XLA Ops:
  0.6 90.8 %join_rows.1 = (bf16[512,128]{1,0:T(8,128)(2,1)}, bf16[2,128]{1,0:T(2,128)(2,1)}, f32[4,128]{1,0:T(4,128)}) custom-call(s32[64,128]{1,0:T(8,128)} %bitcast.5, bf16[8192,128]{1,0:T(8,128)(2,1)} %x_ref.1, s32[1024,128]{1,0:T(8,128)} %bitcast.4, s32[4,128]{1,0:T(4,128)} %bitcast.6, s32[512]{0:T(512)} %heavy_ref.1, bf16[512,128]{1,0:T(8,128)(2,1)} %orders_ref.1), custom_call_target="tpu_custom_call" | custom-call | tf_op jit(solution)/shard_map/join_rows/pallas_call | solution.py:448
  91.4 1.6 %hand_on.1 = (bf16[512,128]{1,0:T(8,128)(2,1)}, bf16[2,128]{1,0:T(2,128)(2,1)}, f32[4,128]{1,0:T(4,128)}) custom-call(bf16[512,128]{1,0:T(8,128)(2,1)} %get-tuple-element.9.a_ref, bf16[2,128]{1,0:T(2,128)(2,1)} %get-tuple-element.10.b_ref, f32[4,128]{1,0:T(4,128)} %get-tuple-element.11.c_ref), custom_call_target="tpu_custom_call" | custom-call | tf_op jit(solution)/shard_map/hand_on/pallas_call | solution.py:504

commit v4 on v3

--- a/solution.py
+++ b/solution.py
@@ -13,8 +13,10 @@
 GX, GY = 64, 4
 KEYS = 131072
 KD = 512
+HK = 256
 OWN = 2048
 CAPK = 64
+HALF = 2048
 HG = 8
 MSG = 80
 LANES = 1024
@@ -67,7 +69,12 @@
         table = jnp.where(lane == k, s, table)
     high = jnp.floor(table * (1.0 / 256.0))
     low = table - 256.0 * high
-    repeat = jnp.where((iota((KD, GX), 0) >> 3) == iota((KD, GX), 1), 1.0, 0.0).astype(BF16)
+    place = iota((KD, GX), 0) >> 3
+    zi = 7 - (place >> 3)
+    dz = ((zi + 1) >> 1) * (1 - 2 * ((zi + 1) & 1))
+    z, x = (me // 2) % 8 + 8 + dz, me // 16 + ((place >> 1) & 3)
+    block = ((x & 3) * 8 + (z & 7)) * 2 + (place & 1)
+    repeat = jnp.where(block == iota((KD, GX), 1), 1.0, 0.0).astype(BF16)
     each = 256.0 * dot(repeat, high.astype(BF16)) + dot(repeat, low.astype(BF16))
     pick = iota((KD, W), 1) == (iota((KD, W), 0) & 7)
     return jnp.sum(jnp.where(pick, each, 0.0), axis=1, keepdims=True).astype(I32)
@@ -83,26 +90,37 @@
     return (((x + 4 + dx) % 4) * 8 + (z + 8 + dz) % 8) * 2
 
 
-def join_kernel(keys_ref, x_ref, ks_ref, hk_ref, heavy_ref, orders_ref,
+def join_kernel(keys_in, x_in, ks_in, hk_in, orders_in,
                 out_ref, report_ref, slots_ref,
-                tab, shi_s, slo_s, seg_s, xe, pt, rk, acc, hq, hx, msg, arr,
+                keys_ref, ks_ref, hk_ref, orders_ref, tab, shi_s, slo_s, seg_s, run_s, xin, xm, xe, pt, rk, acc, ext, cnt_s, slot_s,
+                hq, hx, msg, arr,
                 v_s, meta_s, scol, dense, tal, hsum, hcount, quarters, parts, hquart, hparts,
-                scaled, moved, place_s, ssem, rsem, ysend, yrecv, hsend, hrecv, fsend, frecv, xsem):
+                scaled, moved, place_s, poscol, slots_s, ssem, rsem, ysend, yrecv, hsend, hrecv, fsend, frecv, isem):
     gx, gy = lax.axis_index("gx"), lax.axis_index("gy")
     barrier = pltpu.get_barrier_semaphore()
-    rows_in = pltpu.make_async_copy(x_ref, xe.at[:, 0:W], xsem)
-    rows_in.start()
-
-    def greet(k, carry):
-        pl.semaphore_signal(barrier, inc=1, device_id={"gx": (gx + k) % GX}, device_id_type=MESH)
-        return carry
-
-    lax.fori_loop(1, GX, greet, 0)
+    pairs = ((ks_in, ks_ref), (hk_in, hk_ref), (keys_in, keys_ref), (x_in, xin), (orders_in, orders_ref))
+    inputs = [pltpu.make_async_copy(a, b, isem.at[i]) for i, (a, b) in enumerate(pairs)]
+    for copy in inputs:
+        copy.start()
+
+    def greet(m, carry):
+        for i in range(8):
+            p = pair_at(gx, i // 2, offset(m)) + i % 2
+
+            @pl.when(p != gx)
+            def _():
+                pl.semaphore_signal(barrier, inc=1, device_id={"gx": p}, device_id_type=MESH)
+
+        return carry
+
+    lax.fori_loop(0, 8, greet, 0)
     for k in range(1, GY):
         pl.semaphore_signal(barrier, inc=1, device_id={"gy": (gy + k) % GY}, device_id_type=MESH)
 
     chunks = xe.shape[0] // LANES
     hi_n, lo_n = 512, 256
+    inputs[0].wait()
+    inputs[1].wait()
     for i in range(2):
         ks = ks_ref[pl.ds(i, hi_n, stride=2), :]
         p1 = (ks >> 11) * 2 + ((ks >> 8) & 1)
@@ -142,15 +160,30 @@
         shi = jnp.where(heavy, -1, owner * 8 + ((key >> 9) & 3) * 2 + (a & 1))
         shi_s[pl.ds(c, 1), :] = shi
         slo_s[pl.ds(c, 1), :] = b
-        seg_s[pl.ds(c, 1), :] = jnp.where(
-            heavy, GX * CAPK + (key >> 9) * 2 + jnp.where(second, 1, 0), place * CAPK
-        )
-        pt[...] += dot_t(onehot(lo_n, LANES, 0, b), onehot(hi_n, LANES, 0, shi))
-        return carry
-
+        hid = (key >> 9) * 2 + jnp.where(second, 1, 0)
+        seg_s[pl.ds(c, 1), :] = jnp.where(heavy, HALF + (hid & 255), (place >> 1) * CAPK)
+        run_s[pl.ds(c, 1), :] = jnp.where(heavy, 2 * GX + (hid >> 5), (place >> 5) * CAPK)
+        sub = jnp.where(heavy, hid, place) & 31
+        line = iota((W, LANES), 0)
+        kind = line >> 5
+        facts = jnp.where(kind == 0, 1, jnp.where(kind == 1, b, jnp.where(kind == 2, shi & 7, 0)))
+        facts = jnp.where((line & 31) == sub, facts, 0)
+        at = pl.ds(pl.multiple_of(c * LANES, LANES), LANES)
+        xm[at, :] = facts.astype(F32).T.astype(BF16)
+        side = jnp.where(heavy, hid >> 8, place & 1).astype(F32)
+        sides = jnp.broadcast_to(side, (W, LANES)).T.astype(BF16)
+        x = xin[at, :]
+        right = x * sides
+        xe[at, 0:W] = x - right
+        xe[at, W : 2 * W] = right
+        pt[...] += dot_t(onehot(hi_n, LANES, 0, shi), onehot(lo_n, LANES, 0, b))
+        return carry
+
+    inputs[2].wait()
+    inputs[3].wait()
     lax.fori_loop(0, chunks, look, 0, unroll=2)
 
-    here = jnp.where(pt[...] > 0.5, 1.0, 0.0).astype(BF16)
+    here = jnp.where(pt[...] > 0.5, 1.0, 0.0).T.astype(BF16)
     lower = jnp.where(iota((lo_n, lo_n), 1) < iota((lo_n, lo_n), 0), 1.0, 0.0).astype(BF16)
     r0, r1 = iota((hi_n, hi_n), 0), iota((hi_n, hi_n), 1)
     before = jnp.where((r0 < r1) & ((r0 >> 3) == (r1 >> 3)), 1.0, 0.0).astype(BF16)
@@ -163,31 +196,55 @@
         t = dot(rk[...], onehot(hi_n, LANES, 0, shi))
         mine = iota((lo_n, LANES), 0) == slo
         r = jnp.sum(jnp.where(mine, t, 0.0), axis=0, keepdims=True).astype(I32)
-        seg_s[pl.ds(c, 1), :] = seg_s[pl.ds(c, 1), :] + jnp.where(shi < 0, 0, r)
-        line = iota((W, LANES), 0)
-        ext = jnp.where(line == 0, 1, jnp.where(line == 1, slo, jnp.where(line == 2, shi & 7, 0)))
-        at = pl.ds(pl.multiple_of(c * LANES, LANES), LANES)
-        xe[at, W : 2 * W] = ext.astype(F32).T.astype(BF16)
+        r = jnp.where(shi < 0, 0, r)
+        seg_s[pl.ds(c, 1), :] = seg_s[pl.ds(c, 1), :] + r
+        run_s[pl.ds(c, 1), :] = run_s[pl.ds(c, 1), :] + r
         return carry
 
     lax.fori_loop(0, chunks, rank, 0, unroll=2)
 
-    half = chunks // 2
-
-    def sums(base, c):
+    def sums(base):
         total = None
-        for i in range(half):
-            at = pl.ds(pl.multiple_of((c * half + i) * LANES, LANES), LANES)
-            part = dot(onehot(512, LANES, base, seg_s[pl.ds(c * half + i, 1), :]), xe[at, :])
+        for c in range(chunks):
+            at = slice(c * LANES, (c + 1) * LANES)
+            part = dot(onehot(256, LANES, base, seg_s[c : c + 1, :]), xe[at, :])
             total = part if total is None else total + part
         return total
 
-    rows_in.wait()
+    ext[...] = jnp.zeros_like(ext)
+
+    def gather_facts(c, carry):
+        at = pl.ds(pl.multiple_of(c * LANES, LANES), LANES)
+        ext[...] += dot(onehot(2 * GX + 16, LANES, 0, run_s[pl.ds(c, 1), :]), xm[at, :])
+        return carry
+
+    lax.fori_loop(0, chunks, gather_facts, 0, unroll=4)
+    square = ext[0 : 2 * GX, :].T
+    cnt = square[0:32]
+    slot = jnp.floor((square[32:64] + 256.0 * square[64:96]) / jnp.maximum(cnt, 1.0) + 0.5)
+    slot = jnp.where(cnt > 0.5, slot, -1.0)
+    cnt_s[0:32, :] = cnt.astype(I32)
+    cnt_s[32:64, :] = pltpu.roll(cnt, 64, 1).astype(I32)
+    slot_s[0:32, :] = slot.astype(I32)
+    slot_s[32:64, :] = pltpu.roll(slot, 64, 1).astype(I32)
+
     lane = iota((512, W), 1)
-    acc[...] = sums(GX * CAPK, 0) + sums(GX * CAPK, 1)
-    q, e = encode(acc[:, 0:W])
-    hq[...] = q
-    hx[...] = jnp.where(lane == 64, acc[:, W : W + 1], jnp.where(lane == 65, e, 0.0)).astype(I32)
+    counts = ext[2 * GX : 2 * GX + 16, :]
+    high = jnp.floor(counts * (1.0 / 256.0))
+    spread = jnp.where((iota((512, 16), 0) >> 5) == iota((512, 16), 1), 1.0, 0.0).astype(BF16)
+    each = 256.0 * dot(spread, high.astype(BF16)) + dot(spread, (counts - 256.0 * high).astype(BF16))
+    pick = lane == (iota((512, W), 0) & 31)
+    counts = jnp.sum(jnp.where(pick, each, 0.0), axis=1, keepdims=True)
+
+    def pack_heavy():
+        both = acc[0]
+        q, e = encode(jnp.concatenate([both[:, 0:W], both[:, W : 2 * W]], axis=0))
+        hq[...] = q
+        hx[...] = jnp.where(lane == 64, counts, jnp.where(lane == 65, e, 0.0)).astype(I32)
+
+    acc[...] = jnp.zeros_like(acc)
+    hq[...] = jnp.zeros_like(hq)
+    hx[...] = jnp.zeros_like(hx)
     pl.semaphore_wait(barrier, GX + GY - 2)
 
     def to_owner(o):
@@ -197,59 +254,59 @@
         )
 
     def send(m):
-        def one(i, carry):
+        for i in range(8):
             o = pair_at(gx, i // 2, offset(m)) + i % 2
 
             @pl.when(o != gx)
             def _():
                 to_owner(o).start()
 
-            return carry
-
-        lax.fori_loop(0, 8, one, 0)
-
-    def owners(m, carry):
+    def pack(m, both):
+        q0, e0 = encode(both[:, 0:W])
+        q1, e1 = encode(both[:, W : 2 * W])
+        lane = iota((256, W), 1)
+        e = jnp.where(lane == 0, e0, jnp.where(lane == 1, e1, 0.0)).T[0:8].astype(I32)
         pairs = [pair_at(gx, dx, offset(m)) for dx in range(4)]
-
-        def step(c, carry):
-            @pl.when((c > 0) & (m > 0))
-            def _():
-                send(m - 1)
-
-            acc[...] = jnp.where(c > 0, acc[...], 0.0) + sums(m * 512, c)
-            return carry
-
-        lax.fori_loop(0, 2, step, 0)
-        q, e = encode(acc[:, 0:W])
-        t = jnp.where(lane == 3, e, acc[:, W : 2 * W]).T[0:8]
-        cnt = t[0:1]
-        slot = jnp.where(
-            cnt > 0.5, jnp.floor((t[1:2] + 256.0 * t[2:3]) / jnp.maximum(cnt, 1.0) + 0.5), -1.0
-        )
-        line = iota((8, 512), 0)
-        meta = jnp.where(line == 0, slot, jnp.where(line == 1, cnt, t[3:4])).astype(I32)
+        at = pl.ds(pl.multiple_of(m * 8, 8), 8)
+        slots, counts = slot_s[at, :], cnt_s[at, :]
+        lane, line = iota((8, W), 1), iota((8, W), 0)
         for i in range(8):
             o = pairs[i // 2] + i % 2
-            part = meta[:, (i // 2) * W : (i // 2 + 1) * W]
-            if i % 2:
-                part = pltpu.roll(part, 64, 1)
+            part = e[i % 2 : i % 2 + 1, (i // 4) * W : (i // 4 + 1) * W]
+            exps = pltpu.roll(part, 64, 1) if (i // 2) % 2 else part
+            meta = jnp.where(line == 0, slots[i : i + 1], jnp.where(line == 1, counts[i : i + 1], exps))
             at = pl.ds(pl.multiple_of(o * 8, 8), 8)
-            part = jnp.where(iota((8, W), 1) < 64, part, hx[at, :])
-            values = q[i * 64 : (i + 1) * 64].astype(I16)
-            tail = jnp.concatenate([hq[at, :], part], axis=0).astype(I16)
-            msg[pl.ds(o, 1), 0:64, :] = values[None]
+            meta = jnp.where(lane < 64, meta, hx[at, :])
+            values = (q1 if i % 2 else q0)[(i // 2) * 64 : (i // 2 + 1) * 64]
+            msg[pl.ds(o, 1), 0:64, :] = values.astype(I16)[None]
+            tail = jnp.concatenate([hq[at, :], meta], axis=0).astype(I16)
             msg[pl.ds(o, 1), 64:80, :] = tail[None]
 
-            @pl.when(o == gx)
-            def _():
-                arr[pl.ds(o, 1), 0:64, :] = values[None]
-                arr[pl.ds(o, 1), 64:80, :] = tail[None]
-
-        return carry
-
-    lax.fori_loop(0, 8, owners, 0)
-
-    for q in range(GY):
+    def owners(t, carry):
+        @pl.when(t == 1)
+        def _():
+            pack_heavy()
+
+        @pl.when(t == 2)
+        def _():
+            pack(0, acc[1])
+            scol[0:KD, :] = slots_of(quarter_of(ks_ref, 0), gx)
+            send(0)
+
+        @pl.when(t > 3)
+        def _():
+            send(t - 3)
+
+        pack(jnp.maximum(t - 2, 1), acc[pl.ds((t + 1) % 2, 1), :, :][0])
+        acc[pl.ds(t % 2, 1), :, :] = sums(((t + 8) % 9) * 256)[None]
+        return carry
+
+    lax.fori_loop(0, 9, owners, 0)
+    send(6)
+    pack(7, acc[0])
+    arr[pl.ds(gx, 1), :, :] = msg[pl.ds(gx, 1), :, :]
+
+    for q in range(1, GY):
         at = slice(q * KD, (q + 1) * KD)
         scol[at, :] = slots_of(quarter_of(ks_ref, q), gx) + q * KD
     send(7)
@@ -261,18 +318,24 @@
     lane8 = iota((8, W), 1)
 
     def arrive(m, carry):
+        def wait(i, carry):
+            s = pair_at(gx, -(i // 2), -offset(m)) + i % 2
+
+            @pl.when(s != gx)
+            def _():
+                pltpu.make_async_remote_copy(
+                    src_ref=msg.at[s], dst_ref=arr.at[s], send_sem=ssem.at[s],
+                    recv_sem=rsem.at[s], device_id={"gx": s}, device_id_type=MESH,
+                ).wait_recv()
+
+            return carry
+
+        lax.fori_loop(0, 8, wait, 0)
         for dx in range(4):
             pair = pair_at(gx, -dx, -offset(m))
             metas = []
             for i in range(2):
                 s = pair + i
-
-                @pl.when(s != gx)
-                def _():
-                    pltpu.make_async_remote_copy(
-                        src_ref=msg.at[s], dst_ref=arr.at[s], send_sem=ssem.at[s],
-                        recv_sem=rsem.at[s], device_id={"gx": s}, device_id_type=MESH,
-                    ).wait_recv()
 
                 q = arr[pl.ds(s, 1), 0:64, :][0].astype(I32)
                 high = q >> 8
@@ -311,10 +374,11 @@
         rows = jnp.where(line8 == 3, hcount[2 * q + 1 : 2 * q + 2], rows)
         hquart[q, :, :] = rows
 
-    def to_quarter(p):
+    def to_quarter(h, p):
         return pltpu.make_async_remote_copy(
-            src_ref=quarters.at[p], dst_ref=parts.at[gy], send_sem=ysend.at[p],
-            recv_sem=yrecv.at[gy], device_id={"gy": p}, device_id_type=MESH,
+            src_ref=quarters.at[h * GY + p], dst_ref=parts.at[h * GY + gy],
+            send_sem=ysend.at[h * GY + p], recv_sem=yrecv.at[h * GY + gy],
+            device_id={"gy": p}, device_id_type=MESH,
         )
 
     def heavy_to(p):
@@ -323,37 +387,38 @@
             recv_sem=hrecv.at[gy], device_id={"gy": p}, device_id_type=MESH,
         )
 
-    def leave(k, carry):
+    def leave(n, carry):
+        h, k = n // GY, n % GY + 1
         p = (gy + k) % GY
-        at = pl.ds(pl.multiple_of(p * KD, KD), KD)
+        at = pl.ds(pl.multiple_of(p * KD + h * HK, HK), HK)
         q, e = encode(dense[at, 0:W] * 256.0 + dense[at, W : 2 * W])
         q = q.astype(I16)
         t = jnp.sum(tal[at, :].T, axis=0, keepdims=True)
-        e = jnp.where(lane == 0, e, 0.0).T[0:1]
+        e = jnp.where(iota((HK, W), 1) == 0, e, 0.0).T[0:1]
         line = iota((16, W), 0)
         rows = jnp.zeros((16, W), F32)
-        for i in range(4):
+        for i in range(2):
             rows = jnp.where(line == i, t[:, i * W : (i + 1) * W], rows)
-            rows = jnp.where(line == 4 + i, e[:, i * W : (i + 1) * W], rows)
+            rows = jnp.where(line == 2 + i, e[:, i * W : (i + 1) * W], rows)
         rows = rows.astype(I32).astype(I16)
-        quarters[pl.ds(p, 1), 0:KD, :] = q[None]
-        quarters[pl.ds(p, 1), KD : KD + 16, :] = rows[None]
+        quarters[pl.ds(h * GY + p, 1), 0:HK, :] = q[None]
+        quarters[pl.ds(h * GY + p, 1), HK : HK + 16, :] = rows[None]
 
         @pl.when(k > 1)
         def _():
-            to_quarter((gy + k - 1) % GY).start()
+            to_quarter(h, (gy + k - 1) % GY).start()
 
         @pl.when(k == GY)
         def _():
-            parts[pl.ds(gy, 1), 0:KD, :] = q[None]
-            parts[pl.ds(gy, 1), KD : KD + 16, :] = rows[None]
-
-        return carry
-
-    lax.fori_loop(1, GY + 1, leave, 0)
+            parts[pl.ds(h * GY + gy, 1), 0:HK, :] = q[None]
+            parts[pl.ds(h * GY + gy, 1), HK : HK + 16, :] = rows[None]
+
+        return carry
+
+    lax.fori_loop(0, 2 * GY, leave, 0)
     for k in range(1, GY):
         heavy_to((gy + k) % GY).start()
-    pos = slots_of(quarter_of(ks_ref, gy), gx)
+    poscol[...] = slots_of(quarter_of(ks_ref, gy), gx)
 
     device = gx * GY + gy
     owners_here = [ks_ref[pl.ds(device * 4 + i, 1), :] >> 11 for i in range(4)]
@@ -367,51 +432,67 @@
     w = jnp.sum(jnp.where((row == col) & (j1 < j0), 1.0, 0.0), axis=1, keepdims=True)
     place_s[...] = jnp.where(col * 8 + w.astype(I32) == j1, 1.0, 0.0).astype(BF16)
 
-    total, tallies = jnp.zeros((KD, W), F32), jnp.zeros((W, W), F32)
-    tail = hquart[pl.ds(gy, 1), :, :][0]
-    for k in range(GY):
-        s = (gy + GY - k) % GY
-        if k:
-            for sent, got, ss, rs in ((quarters, parts, ysend, yrecv), (hquart, hparts, hsend, hrecv)):
-                pltpu.make_async_remote_copy(
-                    src_ref=sent.at[s], dst_ref=got.at[s], send_sem=ss.at[s], recv_sem=rs.at[s],
-                    device_id={"gy": s}, device_id_type=MESH,
-                ).wait_recv()
-            tail = tail + hparts[pl.ds(s, 1), :, :][0]
-        rows = parts[pl.ds(s, 1), KD : KD + 16, :][0].astype(F32)
-        square = jnp.concatenate([rows, jnp.zeros((W - 16, W), F32)], axis=0).T
-        scale = jnp.concatenate([square[:, 4 + i : 5 + i] for i in range(4)], axis=0)
-        total = total + parts[pl.ds(s, 1), 0:KD, :][0].astype(F32) * power(scale)
-        tallies = tallies + square
-
-    col = jnp.concatenate([tallies[:, i : i + 1] for i in range(4)], axis=0)
-    scaled[...] = (total * lax.rsqrt(1.0 + col)).reshape(GX, 8, W)
-
-    def to_range(p):
+    def to_range(k, p):
         return pltpu.make_async_remote_copy(
-            src_ref=scaled.at[p], dst_ref=moved.at[gx], send_sem=fsend.at[p],
+            src_ref=scaled.at[k], dst_ref=moved.at[gx], send_sem=fsend.at[p],
             recv_sem=frecv.at[gx], device_id={"gx": p}, device_id_type=MESH,
         )
 
-    slots = jnp.sum(jnp.where(pos == j1, col, 0.0), axis=0, keepdims=True)
+    slots_s[...] = jnp.zeros_like(slots_s)
+
+    def half_quarter(h, carry):
+        total, tallies = jnp.zeros((HK, W), F32), jnp.zeros((W, W), F32)
+        for k in range(1, GY):
+            s = (gy + GY - k) % GY
+            pltpu.make_async_remote_copy(
+                src_ref=quarters.at[h * GY + s], dst_ref=parts.at[h * GY + s],
+                send_sem=ysend.at[h * GY + s], recv_sem=yrecv.at[h * GY + s],
+                device_id={"gy": s}, device_id_type=MESH,
+            ).wait_recv()
+        for s in range(GY):
+            rows = parts[pl.ds(h * GY + s, 1), HK : HK + 16, :][0].astype(F32)
+            square = jnp.concatenate([rows, jnp.zeros((W - 16, W), F32)], axis=0).T
+            scale = jnp.concatenate([square[:, 2 + i : 3 + i] for i in range(2)], axis=0)
+            total = total + parts[pl.ds(h * GY + s, 1), 0:HK, :][0].astype(F32) * power(scale)
+            tallies = tallies + square
+        col = jnp.concatenate([tallies[:, i : i + 1] for i in range(2)], axis=0)
+        at = pl.ds(pl.multiple_of(h * (GX // 2), GX // 2), GX // 2)
+        scaled[at, :, :] = (total * lax.rsqrt(1.0 + col)).reshape(GX // 2, 8, W)
+        pos = poscol[pl.ds(pl.multiple_of(h * HK, HK), HK), :]
+        slots_s[...] += jnp.sum(
+            jnp.where(pos == iota((HK, KD), 1), col, 0.0), axis=0, keepdims=True
+        )
+
+        def range_out(m, carry):
+            for i in range(8):
+                p = pair_at(gx, i // 2, offset(m)) + i % 2
+
+                @pl.when(p != gx)
+                def _():
+                    to_range(m * 8 + i, p).start()
+
+            return carry
+
+        lax.fori_loop(h * 4, h * 4 + 4, range_out, 0)
+        return carry
+
+    lax.fori_loop(0, 2, half_quarter, 0)
+    moved[pl.ds(gx, 1), :, :] = scaled[pl.ds(56 + gx % 2, 1), :, :]
+    slots = slots_s[...]
     slots_ref[...] = jnp.concatenate([slots[:, i * W : (i + 1) * W] for i in range(4)], axis=0)
-
-    def range_out(k, carry):
-        p = pair_at(gx, (k // 2) % 4, offset(k // 8)) + k % 2
-
-        @pl.when(p != gx)
-        def _():
-            to_range(p).start()
-
-        return carry
-
-    lax.fori_loop(0, GX, range_out, 0)
-    moved[pl.ds(gx, 1), :, :] = scaled[pl.ds(gx, 1), :, :]
+    tail = hquart[pl.ds(gy, 1), :, :][0]
+    for k in range(1, GY):
+        s = (gy + GY - k) % GY
+        pltpu.make_async_remote_copy(
+            src_ref=hquart.at[s], dst_ref=hparts.at[s], send_sem=hsend.at[s],
+            recv_sem=hrecv.at[s], device_id={"gy": s}, device_id_type=MESH,
+        ).wait_recv()
+        tail = tail + hparts[pl.ds(s, 1), :, :][0]
 
     def finish(k, carry):
         s = (gx + k) % GX
         to_owner(s).wait_send()
-        to_range(s).wait_send()
+        to_range(s, s).wait_send()
         pltpu.make_async_remote_copy(
             src_ref=scaled.at[s], dst_ref=moved.at[s], send_sem=fsend.at[s],
             recv_sem=frecv.at[s], device_id={"gx": s}, device_id_type=MESH,
@@ -420,9 +501,11 @@
 
     lax.fori_loop(1, GX, finish, 0)
     for k in range(1, GY):
-        to_quarter((gy + k) % GY).wait_send()
+        to_quarter(0, (gy + k) % GY).wait_send()
+        to_quarter(1, (gy + k) % GY).wait_send()
         heavy_to((gy + k) % GY).wait_send()
 
+    inputs[4].wait()
     got = moved[...].reshape(KD, W)
     high = got.astype(BF16)
     low = (got - high.astype(F32)).astype(BF16)
@@ -433,7 +516,9 @@
     line = iota((KD, W), 0)
     reports = []
     for h in range(2):
-        here = line == heavy_ref[2 * device + h] - device * KD
+        ours = iota((1, KD), 1) == 2 * device + h
+        key = jnp.sum(jnp.where(ours, hk, 0).astype(F32), axis=1, keepdims=True).astype(I32)
+        here = line == key - device * KD
         total = jnp.where(here, heavy[h : h + 1, :], total)
         mine = jnp.sum(jnp.where(here, orders, 0.0), axis=0, keepdims=True)
         reports.append(mine * heavy[h : h + 1, :])
@@ -452,20 +537,27 @@
             jax.ShapeDtypeStruct((2, W), BF16),
             jax.ShapeDtypeStruct((4, W), F32),
         ),
-        in_specs=[
-            VMEM, pl.BlockSpec(memory_space=pl.ANY), VMEM, VMEM,
-            pl.BlockSpec(memory_space=pltpu.SMEM), VMEM,
-        ],
+        in_specs=[pl.BlockSpec(memory_space=pl.ANY)] * 5,
         out_specs=(VMEM,) * 3,
         scratch_shapes=[
+            pltpu.VMEM(keys.shape, I32),
+            pltpu.VMEM(ks.shape, I32),
+            pltpu.VMEM(heavy_keys.shape, I32),
+            pltpu.VMEM(orders.shape, BF16),
             pltpu.VMEM((528, 512), BF16),
             pltpu.VMEM((chunks, LANES), I32),
             pltpu.VMEM((chunks, LANES), I32),
             pltpu.VMEM((chunks, LANES), I32),
+            pltpu.VMEM((chunks, LANES), I32),
+            pltpu.VMEM((rows, W), BF16),
+            pltpu.VMEM((rows, W), BF16),
             pltpu.VMEM((rows, 2 * W), BF16),
-            pltpu.VMEM((256, 512), F32),
+            pltpu.VMEM((512, 256), F32),
             pltpu.VMEM((256, 512), BF16),
-            pltpu.VMEM((512, 2 * W), F32),
+            pltpu.VMEM((2, 256, 2 * W), F32),
+            pltpu.VMEM((2 * GX + 16, W), F32),
+            pltpu.VMEM((GX, W), I32),
+            pltpu.VMEM((GX, W), I32),
             pltpu.VMEM((512, W), I32),
             pltpu.VMEM((512, W), I32),
             pltpu.VMEM((GX, MSG, W), I16),
@@ -477,21 +569,23 @@
             pltpu.VMEM((OWN, W), F32),
             pltpu.VMEM((8, W), F32),
             pltpu.VMEM((8, W), F32),
-            pltpu.VMEM((GY, KD + 16, W), I16),
-            pltpu.VMEM((GY, KD + 16, W), I16),
+            pltpu.VMEM((2 * GY, HK + 16, W), I16),
+            pltpu.VMEM((2 * GY, HK + 16, W), I16),
             pltpu.VMEM((GY, 8, W), F32),
             pltpu.VMEM((GY, 8, W), F32),
             pltpu.VMEM((GX, 8, W), F32),
             pltpu.VMEM((GX, 8, W), F32),
             pltpu.VMEM((KD, KD), BF16),
-            dma((GX,)), dma((GX,)), dma((GY,)), dma((GY,)), dma((GY,)), dma((GY,)),
-            dma((GX,)), dma((GX,)), dma,
+            pltpu.VMEM((KD, 1), I32),
+            pltpu.VMEM((1, KD), F32),
+            dma((GX,)), dma((GX,)), dma((2 * GY,)), dma((2 * GY,)), dma((GY,)), dma((GY,)),
+            dma((GX,)), dma((GX,)), dma((5,)),
         ],
         compiler_params=pltpu.CompilerParams(
             collective_id=0, has_side_effects=True, vmem_limit_bytes=56 * 2**20
         ),
         name="join_rows",
-    )(keys, x, ks, heavy_keys.reshape(-1, W), heavy_keys, orders)
+    )(keys, x, ks, heavy_keys, orders)
 
 
 def hand_on_kernel(a_ref, b_ref, c_ref, out_a, out_b, out_c):
@@ -512,7 +606,7 @@
 
 def body(measures, row_keys, orders, heavy_keys, key_slot):
     result, report, slot_rows = join(
-        row_keys.reshape(-1, W), measures, key_slot.reshape(-1, W), heavy_keys, orders
+        row_keys.reshape(-1, W), measures, key_slot.reshape(-1, W), heavy_keys.reshape(-1, W), orders
     )
     result, report, slot_rows = hand_on(result, report, slot_rows)
     return (result, report, slot_rows.reshape(KD))

time: 93.1 us -> 82.6 us (0.89)
  Pallas kernels: 92.4 us -> 81.9 us
    pallas_call x1, Pallas kernels: 90.8 us -> 80.3 us  [join(): pl.pallas_call(join_kernel, out_shape=(jax.ShapeDtypeStruct((KD, W), BF16...]
where the time goes in v4:
time: 82.6 us; the launch traced here: 82.5 us
  Pallas kernels  81.9 us (99%)
    pallas_call x1, Pallas kernels, join(): pl.pallas_call(join_kernel, out_shape=(jax.ShapeDtypeStruct((KD, W), BF16...  80.3 us

profile of v4, /device:TPU:1, one launch (start us, length us, event | category | flops | bytes accessed | tf_op | source)
XLA Modules:
  0.0 82.5 jit_solution(11912725841994069000)
XLA Ops:
  0.6 80.3 %join_rows.1 = (bf16[512,128]{1,0:T(8,128)(2,1)}, bf16[2,128]{1,0:T(2,128)(2,1)}, f32[4,128]{1,0:T(4,128)}) custom-call(s32[64,128]{1,0:T(8,128)} %bitcast.5, bf16[8192,128]{1,0:T(8,128)(2,1)} %x_in.1, s32[1024,128]{1,0:T(8,128)} %bitcast.4, s32[4,128]{1,0:T(4,128)} %bitcast.6, bf16[512,128]{1,0:T(8,128)(2,1)} %orders_in.1), custom_call_target="tpu_custom_call" | custom-call | tf_op jit(solution)/shard_map/join_rows/pallas_call | solution.py:533
  80.9 1.6 %hand_on.1 = (bf16[512,128]{1,0:T(8,128)(2,1)}, bf16[2,128]{1,0:T(2,128)(2,1)}, f32[4,128]{1,0:T(4,128)}) custom-call(bf16[512,128]{1,0:T(8,128)(2,1)} %get-tuple-element.9.a_ref, bf16[2,128]{1,0:T(2,128)(2,1)} %get-tuple-element.10.b_ref, f32[4,128]{1,0:T(4,128)} %get-tuple-element.11.c_ref), custom_call_target="tpu_custom_call" | custom-call | tf_op jit(solution)/shard_map/hand_on/pallas_call | solution.py:598

commit v5 on v4

--- a/solution.py
+++ b/solution.py
@@ -13,7 +13,8 @@
 GX, GY = 64, 4
 KEYS = 131072
 KD = 512
-HK = 256
+HK = 128
+NP = KD // HK
 OWN = 2048
 CAPK = 64
 HALF = 2048
@@ -181,7 +182,7 @@
 
     inputs[2].wait()
     inputs[3].wait()
-    lax.fori_loop(0, chunks, look, 0, unroll=2)
+    lax.fori_loop(0, chunks, look, 0, unroll=4)
 
     here = jnp.where(pt[...] > 0.5, 1.0, 0.0).T.astype(BF16)
     lower = jnp.where(iota((lo_n, lo_n), 1) < iota((lo_n, lo_n), 0), 1.0, 0.0).astype(BF16)
@@ -201,7 +202,7 @@
         run_s[pl.ds(c, 1), :] = run_s[pl.ds(c, 1), :] + r
         return carry
 
-    lax.fori_loop(0, chunks, rank, 0, unroll=2)
+    lax.fori_loop(0, chunks, rank, 0, unroll=4)
 
     def sums(base):
         total = None
@@ -397,9 +398,7 @@
         e = jnp.where(iota((HK, W), 1) == 0, e, 0.0).T[0:1]
         line = iota((16, W), 0)
         rows = jnp.zeros((16, W), F32)
-        for i in range(2):
-            rows = jnp.where(line == i, t[:, i * W : (i + 1) * W], rows)
-            rows = jnp.where(line == 2 + i, e[:, i * W : (i + 1) * W], rows)
+        rows = jnp.where(line == 0, t, jnp.where(line == 1, e, rows))
         rows = rows.astype(I32).astype(I16)
         quarters[pl.ds(h * GY + p, 1), 0:HK, :] = q[None]
         quarters[pl.ds(h * GY + p, 1), HK : HK + 16, :] = rows[None]
@@ -415,7 +414,7 @@
 
         return carry
 
-    lax.fori_loop(0, 2 * GY, leave, 0)
+    lax.fori_loop(0, NP * GY, leave, 0)
     for k in range(1, GY):
         heavy_to((gy + k) % GY).start()
     poscol[...] = slots_of(quarter_of(ks_ref, gy), gx)
@@ -440,7 +439,7 @@
 
     slots_s[...] = jnp.zeros_like(slots_s)
 
-    def half_quarter(h, carry):
+    def piece(h, carry):
         total, tallies = jnp.zeros((HK, W), F32), jnp.zeros((W, W), F32)
         for k in range(1, GY):
             s = (gy + GY - k) % GY
@@ -452,12 +451,12 @@
         for s in range(GY):
             rows = parts[pl.ds(h * GY + s, 1), HK : HK + 16, :][0].astype(F32)
             square = jnp.concatenate([rows, jnp.zeros((W - 16, W), F32)], axis=0).T
-            scale = jnp.concatenate([square[:, 2 + i : 3 + i] for i in range(2)], axis=0)
+            scale = square[:, 1:2]
             total = total + parts[pl.ds(h * GY + s, 1), 0:HK, :][0].astype(F32) * power(scale)
             tallies = tallies + square
-        col = jnp.concatenate([tallies[:, i : i + 1] for i in range(2)], axis=0)
-        at = pl.ds(pl.multiple_of(h * (GX // 2), GX // 2), GX // 2)
-        scaled[at, :, :] = (total * lax.rsqrt(1.0 + col)).reshape(GX // 2, 8, W)
+        col = tallies[:, 0:1]
+        at = pl.ds(h * (GX // NP), GX // NP)
+        scaled[at, :, :] = (total * lax.rsqrt(1.0 + col)).reshape(GX // NP, 8, W)
         pos = poscol[pl.ds(pl.multiple_of(h * HK, HK), HK), :]
         slots_s[...] += jnp.sum(
             jnp.where(pos == iota((HK, KD), 1), col, 0.0), axis=0, keepdims=True
@@ -473,10 +472,10 @@
 
             return carry
 
-        lax.fori_loop(h * 4, h * 4 + 4, range_out, 0)
-        return carry
-
-    lax.fori_loop(0, 2, half_quarter, 0)
+        lax.fori_loop(h * (8 // NP), (h + 1) * (8 // NP), range_out, 0)
+        return carry
+
+    lax.fori_loop(0, NP, piece, 0)
     moved[pl.ds(gx, 1), :, :] = scaled[pl.ds(56 + gx % 2, 1), :, :]
     slots = slots_s[...]
     slots_ref[...] = jnp.concatenate([slots[:, i * W : (i + 1) * W] for i in range(4)], axis=0)
@@ -501,8 +500,8 @@
 
     lax.fori_loop(1, GX, finish, 0)
     for k in range(1, GY):
-        to_quarter(0, (gy + k) % GY).wait_send()
-        to_quarter(1, (gy + k) % GY).wait_send()
+        for h in range(NP):
+            to_quarter(h, (gy + k) % GY).wait_send()
         heavy_to((gy + k) % GY).wait_send()
 
     inputs[4].wait()
@@ -569,8 +568,8 @@
             pltpu.VMEM((OWN, W), F32),
             pltpu.VMEM((8, W), F32),
             pltpu.VMEM((8, W), F32),
-            pltpu.VMEM((2 * GY, HK + 16, W), I16),
-            pltpu.VMEM((2 * GY, HK + 16, W), I16),
+            pltpu.VMEM((NP * GY, HK + 16, W), I16),
+            pltpu.VMEM((NP * GY, HK + 16, W), I16),
             pltpu.VMEM((GY, 8, W), F32),
             pltpu.VMEM((GY, 8, W), F32),
             pltpu.VMEM((GX, 8, W), F32),
@@ -578,7 +577,7 @@
             pltpu.VMEM((KD, KD), BF16),
             pltpu.VMEM((KD, 1), I32),
             pltpu.VMEM((1, KD), F32),
-            dma((GX,)), dma((GX,)), dma((2 * GY,)), dma((2 * GY,)), dma((GY,)), dma((GY,)),
+            dma((GX,)), dma((GX,)), dma((NP * GY,)), dma((NP * GY,)), dma((GY,)), dma((GY,)),
             dma((GX,)), dma((GX,)), dma((5,)),
         ],
         compiler_params=pltpu.CompilerParams(

time: 82.6 us -> 80.6 us (0.976)
  Pallas kernels: 81.9 us -> 79.8 us
    pallas_call x1, Pallas kernels: 80.3 us -> 78.3 us  [join(): pl.pallas_call(join_kernel, out_shape=(jax.ShapeDtypeStruct((KD, W), BF16...]
where the time goes in v5:
time: 80.6 us; the launch traced here: 80.5 us
  Pallas kernels  79.8 us (99%)
    pallas_call x1, Pallas kernels, join(): pl.pallas_call(join_kernel, out_shape=(jax.ShapeDtypeStruct((KD, W), BF16...  78.3 us

profile of v5, /device:TPU:1, one launch (start us, length us, event | category | flops | bytes accessed | tf_op | source)
XLA Modules:
  0.0 80.5 jit_solution(15397338938096091232)
XLA Ops:
  0.6 78.3 %join_rows.1 = (bf16[512,128]{1,0:T(8,128)(2,1)}, bf16[2,128]{1,0:T(2,128)(2,1)}, f32[4,128]{1,0:T(4,128)}) custom-call(s32[64,128]{1,0:T(8,128)} %bitcast.5, bf16[8192,128]{1,0:T(8,128)(2,1)} %x_in.1, s32[1024,128]{1,0:T(8,128)} %bitcast.4, s32[4,128]{1,0:T(4,128)} %bitcast.6, bf16[512,128]{1,0:T(8,128)(2,1)} %orders_in.1), custom_call_target="tpu_custom_call" | custom-call | tf_op jit(solution)/shard_map/join_rows/pallas_call | solution.py:532
  78.9 1.6 %hand_on.1 = (bf16[512,128]{1,0:T(8,128)(2,1)}, bf16[2,128]{1,0:T(2,128)(2,1)}, f32[4,128]{1,0:T(4,128)}) custom-call(bf16[512,128]{1,0:T(8,128)(2,1)} %get-tuple-element.9.a_ref, bf16[2,128]{1,0:T(2,128)(2,1)} %get-tuple-element.10.b_ref, f32[4,128]{1,0:T(4,128)} %get-tuple-element.11.c_ref), custom_call_target="tpu_custom_call" | custom-call | tf_op jit(solution)/shard_map/hand_on/pallas_call | solution.py:597

commit v6 on v5

--- a/solution.py
+++ b/solution.py
@@ -312,6 +312,20 @@
         scol[at, :] = slots_of(quarter_of(ks_ref, q), gx) + q * KD
     send(7)
 
+    poscol[...] = slots_of(quarter_of(ks_ref, gy), gx)
+
+    device = gx * GY + gy
+    owners_here = [ks_ref[pl.ds(device * 4 + i, 1), :] >> 11 for i in range(4)]
+    row = jnp.concatenate(owners_here, axis=1)
+    square = jnp.zeros((W, W), I32)
+    for i in range(4):
+        square = jnp.where(iota((W, W), 0) == i, owners_here[i], square)
+    square = square.astype(F32).T.astype(I32)
+    col = jnp.concatenate([square[:, i : i + 1] for i in range(4)], axis=0)
+    j0, j1 = iota((KD, KD), 0), iota((KD, KD), 1)
+    w = jnp.sum(jnp.where((row == col) & (j1 < j0), 1.0, 0.0), axis=1, keepdims=True)
+    place_s[...] = jnp.where(col * 8 + w.astype(I32) == j1, 1.0, 0.0).astype(BF16)
+
     dense[...] = jnp.zeros_like(dense)
     tal[...] = jnp.zeros_like(tal)
     hsum[...] = jnp.zeros_like(hsum)
@@ -388,9 +402,15 @@
             recv_sem=hrecv.at[gy], device_id={"gy": p}, device_id_type=MESH,
         )
 
+    def piece_at(n):
+        return n // (GY - 1), (gy + n % (GY - 1) + 1) % GY
+
     def leave(n, carry):
-        h, k = n // GY, n % GY + 1
-        p = (gy + k) % GY
+        @pl.when(n > 0)
+        def _():
+            to_quarter(*piece_at(n - 1)).start()
+
+        h, p = piece_at(n)
         at = pl.ds(pl.multiple_of(p * KD + h * HK, HK), HK)
         q, e = encode(dense[at, 0:W] * 256.0 + dense[at, W : 2 * W])
         q = q.astype(I16)
@@ -402,35 +422,12 @@
         rows = rows.astype(I32).astype(I16)
         quarters[pl.ds(h * GY + p, 1), 0:HK, :] = q[None]
         quarters[pl.ds(h * GY + p, 1), HK : HK + 16, :] = rows[None]
-
-        @pl.when(k > 1)
-        def _():
-            to_quarter(h, (gy + k - 1) % GY).start()
-
-        @pl.when(k == GY)
-        def _():
-            parts[pl.ds(h * GY + gy, 1), 0:HK, :] = q[None]
-            parts[pl.ds(h * GY + gy, 1), HK : HK + 16, :] = rows[None]
-
-        return carry
-
-    lax.fori_loop(0, NP * GY, leave, 0)
+        return carry
+
+    lax.fori_loop(0, NP * (GY - 1), leave, 0)
     for k in range(1, GY):
         heavy_to((gy + k) % GY).start()
-    poscol[...] = slots_of(quarter_of(ks_ref, gy), gx)
-
-    device = gx * GY + gy
-    owners_here = [ks_ref[pl.ds(device * 4 + i, 1), :] >> 11 for i in range(4)]
-    row = jnp.concatenate(owners_here, axis=1)
-    square = jnp.zeros((W, W), I32)
-    for i in range(4):
-        square = jnp.where(iota((W, W), 0) == i, owners_here[i], square)
-    square = square.astype(F32).T.astype(I32)
-    col = jnp.concatenate([square[:, i : i + 1] for i in range(4)], axis=0)
-    j0, j1 = iota((KD, KD), 0), iota((KD, KD), 1)
-    w = jnp.sum(jnp.where((row == col) & (j1 < j0), 1.0, 0.0), axis=1, keepdims=True)
-    place_s[...] = jnp.where(col * 8 + w.astype(I32) == j1, 1.0, 0.0).astype(BF16)
-
+    to_quarter(*piece_at(NP * (GY - 1) - 1)).start()
     def to_range(k, p):
         return pltpu.make_async_remote_copy(
             src_ref=scaled.at[k], dst_ref=moved.at[gx], send_sem=fsend.at[p],
@@ -440,7 +437,9 @@
     slots_s[...] = jnp.zeros_like(slots_s)
 
     def piece(h, carry):
-        total, tallies = jnp.zeros((HK, W), F32), jnp.zeros((W, W), F32)
+        at = pl.ds(pl.multiple_of(gy * KD + h * HK, HK), HK)
+        total = dense[at, 0:W] * 256.0 + dense[at, W : 2 * W]
+        col = jnp.sum(tal[at, :], axis=1, keepdims=True)
         for k in range(1, GY):
             s = (gy + GY - k) % GY
             pltpu.make_async_remote_copy(
@@ -448,13 +447,13 @@
                 send_sem=ysend.at[h * GY + s], recv_sem=yrecv.at[h * GY + s],
                 device_id={"gy": s}, device_id_type=MESH,
             ).wait_recv()
-        for s in range(GY):
+        for k in range(1, GY):
+            s = (gy + GY - k) % GY
             rows = parts[pl.ds(h * GY + s, 1), HK : HK + 16, :][0].astype(F32)
             square = jnp.concatenate([rows, jnp.zeros((W - 16, W), F32)], axis=0).T
             scale = square[:, 1:2]
             total = total + parts[pl.ds(h * GY + s, 1), 0:HK, :][0].astype(F32) * power(scale)
-            tallies = tallies + square
-        col = tallies[:, 0:1]
+            col = col + square[:, 0:1]
         at = pl.ds(h * (GX // NP), GX // NP)
         scaled[at, :, :] = (total * lax.rsqrt(1.0 + col)).reshape(GX // NP, 8, W)
         pos = poscol[pl.ds(pl.multiple_of(h * HK, HK), HK), :]

time: 80.6 us -> 80.6 us (level)
  no operation moved by 1% of the time
where the time goes in v6:
time: 80.6 us; the launch traced here: 80.5 us
  Pallas kernels  79.8 us (99%)
    pallas_call x1, Pallas kernels, join(): pl.pallas_call(join_kernel, out_shape=(jax.ShapeDtypeStruct((KD, W), BF16...  78.2 us

profile of v6, /device:TPU:1, one launch (start us, length us, event | category | flops | bytes accessed | tf_op | source)
XLA Modules:
  0.0 80.5 jit_solution(15447061724075680350)
XLA Ops:
  0.6 78.2 %join_rows.1 = (bf16[512,128]{1,0:T(8,128)(2,1)}, bf16[2,128]{1,0:T(2,128)(2,1)}, f32[4,128]{1,0:T(4,128)}) custom-call(s32[64,128]{1,0:T(8,128)} %bitcast.5, bf16[8192,128]{1,0:T(8,128)(2,1)} %x_in.1, s32[1024,128]{1,0:T(8,128)} %bitcast.4, s32[4,128]{1,0:T(4,128)} %bitcast.6, bf16[512,128]{1,0:T(8,128)(2,1)} %orders_in.1), custom_call_target="tpu_custom_call" | custom-call | tf_op jit(solution)/shard_map/join_rows/pallas_call | solution.py:531
  78.9 1.6 %hand_on.1 = (bf16[512,128]{1,0:T(8,128)(2,1)}, bf16[2,128]{1,0:T(2,128)(2,1)}, f32[4,128]{1,0:T(4,128)}) custom-call(bf16[512,128]{1,0:T(8,128)(2,1)} %get-tuple-element.9.a_ref, bf16[2,128]{1,0:T(2,128)(2,1)} %get-tuple-element.10.b_ref, f32[4,128]{1,0:T(4,128)} %get-tuple-element.11.c_ref), custom_call_target="tpu_custom_call" | custom-call | tf_op jit(solution)/shard_map/hand_on/pallas_call | solution.py:596

commit v7 on v5

--- a/solution.py
+++ b/solution.py
@@ -475,7 +475,18 @@
         lax.fori_loop(h * (8 // NP), (h + 1) * (8 // NP), range_out, 0)
         return carry
 
+    def owners_sent(k, carry):
+        to_owner((gx + k) % GX).wait_send()
+        return carry
+
+    def ranges_sent(k, carry):
+        s = (gx + k) % GX
+        to_range(s, s).wait_send()
+        return carry
+
+    lax.fori_loop(1, GX, owners_sent, 0)
     lax.fori_loop(0, NP, piece, 0)
+    lax.fori_loop(1, GX, ranges_sent, 0)
     moved[pl.ds(gx, 1), :, :] = scaled[pl.ds(56 + gx % 2, 1), :, :]
     slots = slots_s[...]
     slots_ref[...] = jnp.concatenate([slots[:, i * W : (i + 1) * W] for i in range(4)], axis=0)
@@ -490,8 +501,6 @@
 
     def finish(k, carry):
         s = (gx + k) % GX
-        to_owner(s).wait_send()
-        to_range(s, s).wait_send()
         pltpu.make_async_remote_copy(
             src_ref=scaled.at[s], dst_ref=moved.at[s], send_sem=fsend.at[s],
             recv_sem=frecv.at[s], device_id={"gx": s}, device_id_type=MESH,

time: 80.6 us -> 80.5 us (level)
  no operation moved by 1% of the time
where the time goes in v7:
time: 80.5 us; the launch traced here: 80.4 us
  Pallas kernels  79.7 us (99%)
    pallas_call x1, Pallas kernels, join(): pl.pallas_call(join_kernel, out_shape=(jax.ShapeDtypeStruct((KD, W), BF16...  78.2 us

profile of v7, /device:TPU:1, one launch (start us, length us, event | category | flops | bytes accessed | tf_op | source)
XLA Modules:
  0.0 80.4 jit_solution(1233584838201770958)
XLA Ops:
  0.6 78.2 %join_rows.1 = (bf16[512,128]{1,0:T(8,128)(2,1)}, bf16[2,128]{1,0:T(2,128)(2,1)}, f32[4,128]{1,0:T(4,128)}) custom-call(s32[64,128]{1,0:T(8,128)} %bitcast.5, bf16[8192,128]{1,0:T(8,128)(2,1)} %x_in.1, s32[1024,128]{1,0:T(8,128)} %bitcast.4, s32[4,128]{1,0:T(4,128)} %bitcast.6, bf16[512,128]{1,0:T(8,128)(2,1)} %orders_in.1), custom_call_target="tpu_custom_call" | custom-call | tf_op jit(solution)/shard_map/join_rows/pallas_call | solution.py:541
  78.8 1.6 %hand_on.1 = (bf16[512,128]{1,0:T(8,128)(2,1)}, bf16[2,128]{1,0:T(2,128)(2,1)}, f32[4,128]{1,0:T(4,128)}) custom-call(bf16[512,128]{1,0:T(8,128)(2,1)} %get-tuple-element.9.a_ref, bf16[2,128]{1,0:T(2,128)(2,1)} %get-tuple-element.10.b_ref, f32[4,128]{1,0:T(4,128)} %get-tuple-element.11.c_ref), custom_call_target="tpu_custom_call" | custom-call | tf_op jit(solution)/shard_map/hand_on/pallas_call | solution.py:606
